TPU v7x, 128 devices: a whole 4x4x4 slice. The times are simulated.
128 devices in a mesh: grp: 4 (over y), gx: 8 (over x_hi, z), gy: 4 (over x_lo, core).
Axes of the slice: x: 4 (x_hi: 2, x_lo: 2; x = x_hi * 2 + x_lo), y: 4, z: 4, core: 2. Of those that a mesh axis runs over, the one named last changes fastest.
Arguments:
- terminal: float32 [4, 32, 64, 512], P(None, 'gx', 'gy', 'grp'), may hold values from -6 to 6
- diffusion: float32 [4], replicated, may hold values from 0.03 to 0.1
- velocity: float32 [32, 64, 512], P('gx', 'gy', 'grp'), may hold values from 0.02 to 0.3
- material: int32 [32, 64, 512], P('gx', 'gy', 'grp'), may hold values from 0 to 7
- rates: float32 [8, 8], replicated, may hold values from 0.005 to 0.04
- stoich: int32 [8, 4], replicated, may hold values from -1 to 1
- plan: int32 [8], replicated, may hold values from 0 to 15, as said below
- basis: bfloat16 [4, 32, 64, 512, 256], P('grp', 'gx', 'gy')
Outputs:
- coefficients: float32 [8, 256], replicated
- adjoint: float32 [4, 32, 64, 512], P(None, 'gx', 'gy', 'grp')
Inputs may be any that keep to these rules, and one draw needn't show every extreme that they name: `plan`: 8 different step numbers in increasing order.
All inputs are finite; a program needn't handle non-finite values.
Results may differ from a plain program's by a relative error of at most 0.0045.
Values sent between devices are 32-bit elements; how exact they have to be, the bound alone decides.
A program may use at most 64 MiB of HBM per device.

v0:
```python
import functools

import jax
import jax.numpy as jnp
from jax import lax
from jax.sharding import Mesh
from jax.sharding import PartitionSpec as P

STEPS = 16
GRP_GX_GY = ("grp", "gx_0", "gx_1", "gy_0", "gy_1")
GX = ("gx_0", "gx_1")
GY = ("gy_0", "gy_1")


def padded_2(value, sides, width):
    for axis, dim in sides:
        count, length = (lax.axis_size(axis), value.shape[dim])
        up = [(i, (i + 1) % count) for i in range(count - 1)]
        down = [(j, i) for i, j in up]
        last = lax.slice_in_dim(value, length - width, length, axis=dim)
        leading = lax.slice_in_dim(value, 0, width, axis=dim)
        before = lax.ppermute(last, axis, up)
        after = lax.ppermute(leading, axis, down)
        value = jnp.concatenate([before, value, after], axis=dim)
    return value


def by_axis(value, axes):
    return functools.reduce(lax.psum, axes, value)


def reaction_table(rates, stoich):
    react_count, spec = stoich.shape
    owner = jnp.arange(react_count) % spec
    pick = (owner[:, None] == jnp.arange(spec)[None, :]).astype(jnp.float32)
    return jnp.einsum(
        "mr,ra,rs->mas", rates, pick, stoich.astype(jnp.float32), precision=lax.Precision.HIGHEST
    )


def advance(padded, diffusion, velocity, react):
    center = padded[:, 1:-1, 1:-1, 1:-1]
    ahead = padded[:, 2:, 1:-1, 1:-1]
    beside = ahead + padded[:, :-2, 1:-1, 1:-1]
    beside = beside + padded[:, 1:-1, 2:, 1:-1] + padded[:, 1:-1, :-2, 1:-1]
    beside = beside + padded[:, 1:-1, 1:-1, 2:] + padded[:, 1:-1, 1:-1, :-2]
    spec = center.shape[0]
    sources = []
    for first in range(spec):
        total = react[first * spec] * center[0]
        for second in range(1, spec):
            total = total + react[first * spec + second] * center[second]
        sources.append(total)
    source = jnp.stack(sources)
    return (
        center
        + diffusion[:, None, None, None] * (beside - 6.0 * center)
        + velocity[None] * (ahead - center)
        + source
    )


def body(terminal, diffusion, velocity, material, rates, stoich, plan, basis):
    spec, cells_x, cells_y, cells_z = terminal.shape
    kinds_count = rates.shape[0]
    table = reaction_table(rates, stoich).reshape(kinds_count, spec * spec)
    kinds = jnp.arange(kinds_count, dtype=jnp.int32)
    onehot = (material.reshape(1, -1) == kinds[:, None]).astype(jnp.float32)
    react = jnp.dot(table.T, onehot, precision=lax.Precision.HIGHEST).reshape(
        spec * spec, cells_x, cells_y, cells_z
    )
    snaps_start = jnp.zeros((plan.shape[0],) + terminal.shape, jnp.float32)

    def keep(snaps, lam, index):
        hit = (plan == index).reshape(-1, 1, 1, 1, 1)
        return jnp.where(hit, lam[None], snaps)

    inside = jnp.ones((1, cells_x, cells_y, cells_z), jnp.float32)
    coeffs = jnp.concatenate([velocity[None], inside, react], 0)
    rim = padded_2(coeffs, (("grp", 3), (GX, 1), (GY, 2)), 1)

    def pair_step(turn, carry):
        lam, snaps = carry
        padded = padded_2(lam, (("grp", 3), (GX, 1), (GY, 2)), 2)
        middle = advance(padded, diffusion, rim[0], rim[2:]) * rim[1][None]
        lam = advance(middle, diffusion, velocity, react)
        snaps = keep(snaps, middle[:, 1:-1, 1:-1, 1:-1], 2 * turn)
        snaps = keep(snaps, lam, 2 * turn + 1)
        return (lam, snaps)

    final, snaps = lax.fori_loop(0, STEPS // 2, pair_step, (terminal, snaps_start))
    moved = lax.all_to_all(snaps, "grp", split_axis=1, concat_axis=4, tiled=True)
    flat = moved.reshape(moved.shape[0], -1)
    local = basis.reshape(-1, basis.shape[-1])
    first = by_axis(
        jnp.dot(flat.astype(jnp.bfloat16), local, preferred_element_type=jnp.float32), GRP_GX_GY
    )
    proj = lax.dot_general(
        first.astype(jnp.bfloat16),
        local,
        (((1,), (1,)), ((), ())),
        preferred_element_type=jnp.float32,
    )
    rest = flat - proj
    second = by_axis(
        jnp.dot(rest.astype(jnp.bfloat16), local, preferred_element_type=jnp.float32), GRP_GX_GY
    )
    return (first + second, final)


def solution(mesh):
    split = Mesh(
        mesh.devices.reshape(mesh.shape["grp"], 2, 4, 2, 2), ("grp", "gx_0", "gx_1", "gy_0", "gy_1")
    )
    return jax.shard_map(
        body,
        mesh=split,
        in_specs=(
            P(None, GX, GY, "grp"),
            P(),
            P(GX, GY, "grp"),
            P(GX, GY, "grp"),
            P(),
            P(),
            P(),
            P("grp", GX, GY, None, None),
        ),
        out_specs=(P(), P(None, GX, GY, "grp")),
        check_vma=False,
    )
```

profile of v0, /device:TPU:6, one launch (start us, length us, event | category | flops | bytes accessed | tf_op | source)
XLA Modules:
  0.0 433.1 jit_solution(3957766115090777281)
XLA Ops:
  10.1 4.0 collective-permute-done.7
  19.1 5.6 %collective-permute-start.9 = (f32[18,1,16,130]{3,0,2,1:T(8,128)S(1)}, f32[18,1,16,130]{3,0,2,1:T(8,128)S(1)}, u32[]{:S(2)}, u32[]{:S(2)}) collective-permute-start(f32[18,1,16,130]{3,0,2,1:T(8,128)S(1)} %get-tuple-element.236), channel_id=1, source_target_pairs={{4,0},{8,4},{12,8},{16,12},{20,16},{24,20},{28,24},{5,1},{9,5},{13... | collective-permute-start | bytes 449288 | tf_op jit(solution)/shard_map/ppermute | solution.py:23
  24.7 5.5 %collective-permute-done.8 = f32[18,1,16,130]{3,0,2,1:T(8,128)S(1)} collective-permute-done((f32[18,1,16,130]{3,0,2,1:T(8,128)S(1)}, f32[18,1,16,130]{3,0,2,1:T(8,128)S(1)}, u32[]{:S(2)}, u32[]{:S(2)}) %collective-permute-start.8) | collective-permute-done | bytes 149792 | tf_op jit(solution)/shard_map/ppermute | solution.py:22
  42.5 278.7 %while.16 = (s32[]{:T(128)}, f32[4,4,16,128]{3,2,1,0:T(8,128)S(1)}, f32[8,4,4,16,128]{4,3,2,1,0:T(8,128)}, f32[4]{0:T(128)S(1)}, f32[18,6,18,130]{3,2,1,0:T(8,12...) while((s32[]{:T(128)}, f32[4,4,16,128]{3,2,1,0:T(8,128)S(1)}, ...), condition=%wide.region_1.2_spmd.clone, body=%wide.region_0.1_spmd.clone.sunk | while | flops 4091605 | bytes 21316484 | solution.py:91
  43.9 4.6 %collective-permute-start.1 = (f32[4,4,16,2]{3,2,1,0:T(8,128)S(1)}, f32[4,4,16,2]{3,2,1,0:T(8,128)S(1)}, u32[]{:S(2)}, u32[]{:S(2)}) collective-permute-start(f32[4,4,16,2]{3,2,1,0:T(8,128)S(1)} %get-tuple-element.309), channel_id=1, source_target_pairs={{0,32},{32,64},{64,96},{1,33},{33,65},{65,97},{2,34},{34,66},{66,9... | collective-permute-start | bytes 6152 | tf_op jit(solution)/shard_map/while/body/eval_jaxpr/ppermute | solution.py:22
  51.8 8.0 %collective-permute-start.2 = (f32[4,2,16,132]{3,2,1,0:T(8,128)}, f32[4,2,16,132]{3,2,1,0:T(8,128)S(1)}, u32[]{:S(2)}, u32[]{:S(2)}) collective-permute-start(f32[4,2,16,132]{3,2,1,0:T(8,128)} %get-tuple-element.310), channel_id=1, source_target_pairs={{4,0},{8,4},{12,8},{16,12},{20,16},{24,20},{28,24},{5,1},{9,5},{13... | collective-permute-start | bytes 202760 | tf_op jit(solution)/shard_map/while/body/eval_jaxpr/ppermute | solution.py:23
  62.6 7.7 %collective-permute-done.3 = f32[4,2,16,132]{3,2,1,0:T(8,128)S(1)} collective-permute-done((f32[4,2,16,132]{3,2,1,0:T(8,128)S(1)}, f32[4,2,16,132]{3,2,1,0:T(8,128)S(1)}, u32[]{:S(2)}, u32[]{:S(2)}) %collective-permute-start.3) | collective-permute-done | bytes 67616 | tf_op jit(solution)/shard_map/while/body/eval_jaxpr/ppermute | solution.py:22
  83.7 5.0 %collective-permute-start.1 = (f32[4,4,16,2]{3,2,1,0:T(8,128)S(1)}, f32[4,4,16,2]{3,2,1,0:T(8,128)S(1)}, u32[]{:S(2)}, u32[]{:S(2)}) collective-permute-start(f32[4,4,16,2]{3,2,1,0:T(8,128)S(1)} %get-tuple-element.309), channel_id=1, source_target_pairs={{0,32},{32,64},{64,96},{1,33},{33,65},{65,97},{2,34},{34,66},{66,9... | collective-permute-start | bytes 6152 | tf_op jit(solution)/shard_map/while/body/eval_jaxpr/ppermute | solution.py:22
  99.1 5.3 %collective-permute-done.3 = f32[4,2,16,132]{3,2,1,0:T(8,128)S(1)} collective-permute-done((f32[4,2,16,132]{3,2,1,0:T(8,128)S(1)}, f32[4,2,16,132]{3,2,1,0:T(8,128)S(1)}, u32[]{:S(2)}, u32[]{:S(2)}) %collective-permute-start.3) | collective-permute-done | bytes 67616 | tf_op jit(solution)/shard_map/while/body/eval_jaxpr/ppermute | solution.py:22
  117.8 5.0 %collective-permute-start.1 = (f32[4,4,16,2]{3,2,1,0:T(8,128)S(1)}, f32[4,4,16,2]{3,2,1,0:T(8,128)S(1)}, u32[]{:S(2)}, u32[]{:S(2)}) collective-permute-start(f32[4,4,16,2]{3,2,1,0:T(8,128)S(1)} %get-tuple-element.309), channel_id=1, source_target_pairs={{0,32},{32,64},{64,96},{1,33},{33,65},{65,97},{2,34},{34,66},{66,9... | collective-permute-start | bytes 6152 | tf_op jit(solution)/shard_map/while/body/eval_jaxpr/ppermute | solution.py:22
  133.2 5.3 %collective-permute-done.3 = f32[4,2,16,132]{3,2,1,0:T(8,128)S(1)} collective-permute-done((f32[4,2,16,132]{3,2,1,0:T(8,128)S(1)}, f32[4,2,16,132]{3,2,1,0:T(8,128)S(1)}, u32[]{:S(2)}, u32[]{:S(2)}) %collective-permute-start.3) | collective-permute-done | bytes 67616 | tf_op jit(solution)/shard_map/while/body/eval_jaxpr/ppermute | solution.py:22
  151.9 5.0 %collective-permute-start.1 = (f32[4,4,16,2]{3,2,1,0:T(8,128)S(1)}, f32[4,4,16,2]{3,2,1,0:T(8,128)S(1)}, u32[]{:S(2)}, u32[]{:S(2)}) collective-permute-start(f32[4,4,16,2]{3,2,1,0:T(8,128)S(1)} %get-tuple-element.309), channel_id=1, source_target_pairs={{0,32},{32,64},{64,96},{1,33},{33,65},{65,97},{2,34},{34,66},{66,9... | collective-permute-start | bytes 6152 | tf_op jit(solution)/shard_map/while/body/eval_jaxpr/ppermute | solution.py:22
  167.3 5.3 %collective-permute-done.3 = f32[4,2,16,132]{3,2,1,0:T(8,128)S(1)} collective-permute-done((f32[4,2,16,132]{3,2,1,0:T(8,128)S(1)}, f32[4,2,16,132]{3,2,1,0:T(8,128)S(1)}, u32[]{:S(2)}, u32[]{:S(2)}) %collective-permute-start.3) | collective-permute-done | bytes 67616 | tf_op jit(solution)/shard_map/while/body/eval_jaxpr/ppermute | solution.py:22
  186.0 5.0 %collective-permute-start.1 = (f32[4,4,16,2]{3,2,1,0:T(8,128)S(1)}, f32[4,4,16,2]{3,2,1,0:T(8,128)S(1)}, u32[]{:S(2)}, u32[]{:S(2)}) collective-permute-start(f32[4,4,16,2]{3,2,1,0:T(8,128)S(1)} %get-tuple-element.309), channel_id=1, source_target_pairs={{0,32},{32,64},{64,96},{1,33},{33,65},{65,97},{2,34},{34,66},{66,9... | collective-permute-start | bytes 6152 | tf_op jit(solution)/shard_map/while/body/eval_jaxpr/ppermute | solution.py:22
  201.4 5.3 %collective-permute-done.3 = f32[4,2,16,132]{3,2,1,0:T(8,128)S(1)} collective-permute-done((f32[4,2,16,132]{3,2,1,0:T(8,128)S(1)}, f32[4,2,16,132]{3,2,1,0:T(8,128)S(1)}, u32[]{:S(2)}, u32[]{:S(2)}) %collective-permute-start.3) | collective-permute-done | bytes 67616 | tf_op jit(solution)/shard_map/while/body/eval_jaxpr/ppermute | solution.py:22
  220.2 5.0 %collective-permute-start.1 = (f32[4,4,16,2]{3,2,1,0:T(8,128)S(1)}, f32[4,4,16,2]{3,2,1,0:T(8,128)S(1)}, u32[]{:S(2)}, u32[]{:S(2)}) collective-permute-start(f32[4,4,16,2]{3,2,1,0:T(8,128)S(1)} %get-tuple-element.309), channel_id=1, source_target_pairs={{0,32},{32,64},{64,96},{1,33},{33,65},{65,97},{2,34},{34,66},{66,9... | collective-permute-start | bytes 6152 | tf_op jit(solution)/shard_map/while/body/eval_jaxpr/ppermute | solution.py:22
  235.6 5.3 %collective-permute-done.3 = f32[4,2,16,132]{3,2,1,0:T(8,128)S(1)} collective-permute-done((f32[4,2,16,132]{3,2,1,0:T(8,128)S(1)}, f32[4,2,16,132]{3,2,1,0:T(8,128)S(1)}, u32[]{:S(2)}, u32[]{:S(2)}) %collective-permute-start.3) | collective-permute-done | bytes 67616 | tf_op jit(solution)/shard_map/while/body/eval_jaxpr/ppermute | solution.py:22
  254.3 5.0 %collective-permute-start.1 = (f32[4,4,16,2]{3,2,1,0:T(8,128)S(1)}, f32[4,4,16,2]{3,2,1,0:T(8,128)S(1)}, u32[]{:S(2)}, u32[]{:S(2)}) collective-permute-start(f32[4,4,16,2]{3,2,1,0:T(8,128)S(1)} %get-tuple-element.309), channel_id=1, source_target_pairs={{0,32},{32,64},{64,96},{1,33},{33,65},{65,97},{2,34},{34,66},{66,9... | collective-permute-start | bytes 6152 | tf_op jit(solution)/shard_map/while/body/eval_jaxpr/ppermute | solution.py:22
  269.7 5.3 %collective-permute-done.3 = f32[4,2,16,132]{3,2,1,0:T(8,128)S(1)} collective-permute-done((f32[4,2,16,132]{3,2,1,0:T(8,128)S(1)}, f32[4,2,16,132]{3,2,1,0:T(8,128)S(1)}, u32[]{:S(2)}, u32[]{:S(2)}) %collective-permute-start.3) | collective-permute-done | bytes 67616 | tf_op jit(solution)/shard_map/while/body/eval_jaxpr/ppermute | solution.py:22
  288.4 5.0 %collective-permute-start.1 = (f32[4,4,16,2]{3,2,1,0:T(8,128)S(1)}, f32[4,4,16,2]{3,2,1,0:T(8,128)S(1)}, u32[]{:S(2)}, u32[]{:S(2)}) collective-permute-start(f32[4,4,16,2]{3,2,1,0:T(8,128)S(1)} %get-tuple-element.309), channel_id=1, source_target_pairs={{0,32},{32,64},{64,96},{1,33},{33,65},{65,97},{2,34},{34,66},{66,9... | collective-permute-start | bytes 6152 | tf_op jit(solution)/shard_map/while/body/eval_jaxpr/ppermute | solution.py:22
  303.8 5.3 %collective-permute-done.3 = f32[4,2,16,132]{3,2,1,0:T(8,128)S(1)} collective-permute-done((f32[4,2,16,132]{3,2,1,0:T(8,128)S(1)}, f32[4,2,16,132]{3,2,1,0:T(8,128)S(1)}, u32[]{:S(2)}, u32[]{:S(2)}) %collective-permute-start.3) | collective-permute-done | bytes 67616 | tf_op jit(solution)/shard_map/while/body/eval_jaxpr/ppermute | solution.py:22
  322.5 19.4 %all_to_all.15 = f32[8,4,4,16,128]{4,3,2,0,1:T(8,128)S(1)} all-to-all(f32[8,4,4,16,128]{4,3,2,0,1:T(8,128)S(1)} %copy.28), channel_id=1, replica_groups=mesh['grp'=4,'gx_0'=2,'gx_1'=4,'gy_0'=2,'gy_1'=2] {'grp'}, dimensions={1} | all-to-all | bytes 2097152 | tf_op jit(solution)/shard_map/all_to_all | solution.py:92
  344.1 8.0 %fusion.32 = f32[8,256]{1,0:T(8,128)S(1)} fusion(bf16[8,32768]{1,0:T(8,128)(2,1)S(1)} %convert_element_type.19, bf16[32768,256]{1,0:T(8,128)(2,1)} %bitcast.35), kind=kOutput, calls=%fused_computation.88 | convolution fusion | flops 134217728 | bytes 17309696 | tf_op jit(solution)/shard_map/dot_general | solution.py:96
  352.1 9.0 %psum.70 = f32[8,256]{1,0:T(8,128)S(1)} all-reduce(f32[8,256]{1,0:T(8,128)S(1)} %fusion.32), channel_id=1, replica_groups=mesh['grp'=4,'gx_0'=2,'gx_1'=4,'gy_0'=2,'gy_1'=2] {'grp'}, use_global_device_ids=true, to_apply=%region_2.3 | all-reduce | flops 2048 | bytes 16384 | tf_op jit(solution)/shard_map/psum | solution.py:29
  361.1 6.5 %psum.71 = f32[8,256]{1,0:T(8,128)S(1)} all-reduce(f32[8,256]{1,0:T(8,128)S(1)} %psum.70), channel_id=1, replica_groups=mesh['grp'=4,'gx_0'=2,'gx_1'=4,'gy_0'=2,'gy_1'=2] {'gx_0'}, use_global_device_ids=true, to_apply=%region_3.4 | all-reduce | flops 2048 | bytes 16384 | tf_op jit(solution)/shard_map/psum | solution.py:29
  367.6 7.8 %psum.72 = f32[8,256]{1,0:T(8,128)S(1)} all-reduce(f32[8,256]{1,0:T(8,128)S(1)} %psum.71), channel_id=1, replica_groups=mesh['grp'=4,'gx_0'=2,'gx_1'=4,'gy_0'=2,'gy_1'=2] {'gx_1'}, use_global_device_ids=true, to_apply=%region_4.5 | all-reduce | flops 2048 | bytes 16384 | tf_op jit(solution)/shard_map/psum | solution.py:29
  375.5 5.0 %psum.73 = f32[8,256]{1,0:T(8,128)S(1)} all-reduce(f32[8,256]{1,0:T(8,128)S(1)} %psum.72), channel_id=1, replica_groups=mesh['grp'=4,'gx_0'=2,'gx_1'=4,'gy_0'=2,'gy_1'=2] {'gy_0'}, use_global_device_ids=true, to_apply=%region_5.6 | all-reduce | flops 2048 | bytes 16384 | tf_op jit(solution)/shard_map/psum | solution.py:29
  383.0 17.0 %fusion.15 = f32[8,256]{1,0:T(8,128)S(1)} fusion(bf16[32768,256]{1,0:T(8,128)(2,1)} %bitcast.36, f32[8,32768]{1,0:T(8,128)S(1)} %reshape.65, f32[8,256]{1,0:T(8,128)S(1)} %psum.74), kind=kOutput, calls=%fused_computation.57 | convolution fusion | flops 268961792 | bytes 17842176 | tf_op jit(solution)/shard_map/dot_general | solution.py:106
  400.0 8.7 %psum.75 = f32[8,256]{1,0:T(8,128)S(1)} all-reduce(f32[8,256]{1,0:T(8,128)S(1)} %fusion.15), channel_id=1, replica_groups=mesh['grp'=4,'gx_0'=2,'gx_1'=4,'gy_0'=2,'gy_1'=2] {'grp'}, use_global_device_ids=true, to_apply=%region_7.8 | all-reduce | flops 2048 | bytes 16384 | tf_op jit(solution)/shard_map/psum | solution.py:29
  408.7 6.5 %psum.76 = f32[8,256]{1,0:T(8,128)S(1)} all-reduce(f32[8,256]{1,0:T(8,128)S(1)} %psum.75), channel_id=1, replica_groups=mesh['grp'=4,'gx_0'=2,'gx_1'=4,'gy_0'=2,'gy_1'=2] {'gx_0'}, use_global_device_ids=true, to_apply=%region_8.9 | all-reduce | flops 2048 | bytes 16384 | tf_op jit(solution)/shard_map/psum | solution.py:29
  415.2 9.8 %psum.77 = f32[8,256]{1,0:T(8,128)S(1)} all-reduce(f32[8,256]{1,0:T(8,128)S(1)} %psum.76), channel_id=1, replica_groups=mesh['grp'=4,'gx_0'=2,'gx_1'=4,'gy_0'=2,'gy_1'=2] {'gx_1'}, use_global_device_ids=true, to_apply=%region_9.10 | all-reduce | flops 2048 | bytes 16384 | tf_op jit(solution)/shard_map/psum | solution.py:29
  425.0 5.0 %psum.78 = f32[8,256]{1,0:T(8,128)S(1)} all-reduce(f32[8,256]{1,0:T(8,128)S(1)} %psum.77), channel_id=1, replica_groups=mesh['grp'=4,'gx_0'=2,'gx_1'=4,'gy_0'=2,'gy_1'=2] {'gy_0'}, use_global_device_ids=true, to_apply=%region_10.11 | all-reduce | flops 2048 | bytes 16384 | tf_op jit(solution)/shard_map/psum | solution.py:29
  (278 shorter events, 220.5 us)
Async XLA Ops:
  15.2 14.9 %collective-permute-start.8 = (f32[18,1,16,130]{3,0,2,1:T(8,128)S(1)}, f32[18,1,16,130]{3,0,2,1:T(8,128)S(1)}, u32[]{:S(2)}, u32[]{:S(2)}) collective-permute-start(f32[18,1,16,130]{3,0,2,1:T(8,128)S(1)} %get-tuple-element.235), channel_id=1, source_target_pairs={{0,4},{4,8},{8,12},{12,16},{16,20},{20,24},{24,28},{1,5},{5,9},{9,... | collective-permute-start | bytes 449288 | tf_op jit(solution)/shard_map/ppermute | solution.py:22
  19.1 12.3 %collective-permute-start.9 = (f32[18,1,16,130]{3,0,2,1:T(8,128)S(1)}, f32[18,1,16,130]{3,0,2,1:T(8,128)S(1)}, u32[]{:S(2)}, u32[]{:S(2)}) collective-permute-start(f32[18,1,16,130]{3,0,2,1:T(8,128)S(1)} %get-tuple-element.236), channel_id=1, source_target_pairs={{4,0},{8,4},{12,8},{16,12},{20,16},{24,20},{28,24},{5,1},{9,5},{13... | collective-permute-start | bytes 449288 | tf_op jit(solution)/shard_map/ppermute | solution.py:23
  51.8 10.8 %collective-permute-start.2 = (f32[4,2,16,132]{3,2,1,0:T(8,128)}, f32[4,2,16,132]{3,2,1,0:T(8,128)S(1)}, u32[]{:S(2)}, u32[]{:S(2)}) collective-permute-start(f32[4,2,16,132]{3,2,1,0:T(8,128)} %get-tuple-element.310), channel_id=1, source_target_pairs={{4,0},{8,4},{12,8},{16,12},{20,16},{24,20},{28,24},{5,1},{9,5},{13... | collective-permute-start | bytes 202760 | tf_op jit(solution)/shard_map/while/body/eval_jaxpr/ppermute | solution.py:23
  59.8 10.5 %collective-permute-start.3 = (f32[4,2,16,132]{3,2,1,0:T(8,128)S(1)}, f32[4,2,16,132]{3,2,1,0:T(8,128)S(1)}, u32[]{:S(2)}, u32[]{:S(2)}) collective-permute-start(f32[4,2,16,132]{3,2,1,0:T(8,128)S(1)} %get-tuple-element.311), channel_id=1, source_target_pairs={{0,4},{4,8},{8,12},{12,16},{16,20},{20,24},{24,28},{1,5},{5,9},{9,... | collective-permute-start | bytes 202760 | tf_op jit(solution)/shard_map/while/body/eval_jaxpr/ppermute | solution.py:22
  82.4 7.3 %collective-permute-start = (f32[4,4,16,2]{3,2,1,0:T(8,128)S(1)}, f32[4,4,16,2]{3,2,1,0:T(8,128)S(1)}, u32[]{:S(2)}, u32[]{:S(2)}) collective-permute-start(f32[4,4,16,2]{3,2,1,0:T(8,128)S(1)} %get-tuple-element.308), channel_id=1, source_target_pairs={{32,0},{64,32},{96,64},{33,1},{65,33},{97,65},{34,2},{66,34},{98,6... | collective-permute-start | bytes 6152 | tf_op jit(solution)/shard_map/while/body/eval_jaxpr/ppermute | solution.py:23
  83.7 7.5 %collective-permute-start.1 = (f32[4,4,16,2]{3,2,1,0:T(8,128)S(1)}, f32[4,4,16,2]{3,2,1,0:T(8,128)S(1)}, u32[]{:S(2)}, u32[]{:S(2)}) collective-permute-start(f32[4,4,16,2]{3,2,1,0:T(8,128)S(1)} %get-tuple-element.309), channel_id=1, source_target_pairs={{0,32},{32,64},{64,96},{1,33},{33,65},{65,97},{2,34},{34,66},{66,9... | collective-permute-start | bytes 6152 | tf_op jit(solution)/shard_map/while/body/eval_jaxpr/ppermute | solution.py:22
  92.0 7.1 %collective-permute-start.2 = (f32[4,2,16,132]{3,2,1,0:T(8,128)}, f32[4,2,16,132]{3,2,1,0:T(8,128)S(1)}, u32[]{:S(2)}, u32[]{:S(2)}) collective-permute-start(f32[4,2,16,132]{3,2,1,0:T(8,128)} %get-tuple-element.310), channel_id=1, source_target_pairs={{4,0},{8,4},{12,8},{16,12},{20,16},{24,20},{28,24},{5,1},{9,5},{13... | collective-permute-start | bytes 202760 | tf_op jit(solution)/shard_map/while/body/eval_jaxpr/ppermute | solution.py:23
  93.9 10.5 %collective-permute-start.3 = (f32[4,2,16,132]{3,2,1,0:T(8,128)S(1)}, f32[4,2,16,132]{3,2,1,0:T(8,128)S(1)}, u32[]{:S(2)}, u32[]{:S(2)}) collective-permute-start(f32[4,2,16,132]{3,2,1,0:T(8,128)S(1)} %get-tuple-element.311), channel_id=1, source_target_pairs={{0,4},{4,8},{8,12},{12,16},{16,20},{20,24},{24,28},{1,5},{5,9},{9,... | collective-permute-start | bytes 202760 | tf_op jit(solution)/shard_map/while/body/eval_jaxpr/ppermute | solution.py:22
  116.5 7.3 %collective-permute-start = (f32[4,4,16,2]{3,2,1,0:T(8,128)S(1)}, f32[4,4,16,2]{3,2,1,0:T(8,128)S(1)}, u32[]{:S(2)}, u32[]{:S(2)}) collective-permute-start(f32[4,4,16,2]{3,2,1,0:T(8,128)S(1)} %get-tuple-element.308), channel_id=1, source_target_pairs={{32,0},{64,32},{96,64},{33,1},{65,33},{97,65},{34,2},{66,34},{98,6... | collective-permute-start | bytes 6152 | tf_op jit(solution)/shard_map/while/body/eval_jaxpr/ppermute | solution.py:23
  117.8 7.5 %collective-permute-start.1 = (f32[4,4,16,2]{3,2,1,0:T(8,128)S(1)}, f32[4,4,16,2]{3,2,1,0:T(8,128)S(1)}, u32[]{:S(2)}, u32[]{:S(2)}) collective-permute-start(f32[4,4,16,2]{3,2,1,0:T(8,128)S(1)} %get-tuple-element.309), channel_id=1, source_target_pairs={{0,32},{32,64},{64,96},{1,33},{33,65},{65,97},{2,34},{34,66},{66,9... | collective-permute-start | bytes 6152 | tf_op jit(solution)/shard_map/while/body/eval_jaxpr/ppermute | solution.py:22
  126.1 7.1 %collective-permute-start.2 = (f32[4,2,16,132]{3,2,1,0:T(8,128)}, f32[4,2,16,132]{3,2,1,0:T(8,128)S(1)}, u32[]{:S(2)}, u32[]{:S(2)}) collective-permute-start(f32[4,2,16,132]{3,2,1,0:T(8,128)} %get-tuple-element.310), channel_id=1, source_target_pairs={{4,0},{8,4},{12,8},{16,12},{20,16},{24,20},{28,24},{5,1},{9,5},{13... | collective-permute-start | bytes 202760 | tf_op jit(solution)/shard_map/while/body/eval_jaxpr/ppermute | solution.py:23
  128.0 10.5 %collective-permute-start.3 = (f32[4,2,16,132]{3,2,1,0:T(8,128)S(1)}, f32[4,2,16,132]{3,2,1,0:T(8,128)S(1)}, u32[]{:S(2)}, u32[]{:S(2)}) collective-permute-start(f32[4,2,16,132]{3,2,1,0:T(8,128)S(1)} %get-tuple-element.311), channel_id=1, source_target_pairs={{0,4},{4,8},{8,12},{12,16},{16,20},{20,24},{24,28},{1,5},{5,9},{9,... | collective-permute-start | bytes 202760 | tf_op jit(solution)/shard_map/while/body/eval_jaxpr/ppermute | solution.py:22
  150.6 7.3 %collective-permute-start = (f32[4,4,16,2]{3,2,1,0:T(8,128)S(1)}, f32[4,4,16,2]{3,2,1,0:T(8,128)S(1)}, u32[]{:S(2)}, u32[]{:S(2)}) collective-permute-start(f32[4,4,16,2]{3,2,1,0:T(8,128)S(1)} %get-tuple-element.308), channel_id=1, source_target_pairs={{32,0},{64,32},{96,64},{33,1},{65,33},{97,65},{34,2},{66,34},{98,6... | collective-permute-start | bytes 6152 | tf_op jit(solution)/shard_map/while/body/eval_jaxpr/ppermute | solution.py:23
  151.9 7.5 %collective-permute-start.1 = (f32[4,4,16,2]{3,2,1,0:T(8,128)S(1)}, f32[4,4,16,2]{3,2,1,0:T(8,128)S(1)}, u32[]{:S(2)}, u32[]{:S(2)}) collective-permute-start(f32[4,4,16,2]{3,2,1,0:T(8,128)S(1)} %get-tuple-element.309), channel_id=1, source_target_pairs={{0,32},{32,64},{64,96},{1,33},{33,65},{65,97},{2,34},{34,66},{66,9... | collective-permute-start | bytes 6152 | tf_op jit(solution)/shard_map/while/body/eval_jaxpr/ppermute | solution.py:22
  160.2 7.1 %collective-permute-start.2 = (f32[4,2,16,132]{3,2,1,0:T(8,128)}, f32[4,2,16,132]{3,2,1,0:T(8,128)S(1)}, u32[]{:S(2)}, u32[]{:S(2)}) collective-permute-start(f32[4,2,16,132]{3,2,1,0:T(8,128)} %get-tuple-element.310), channel_id=1, source_target_pairs={{4,0},{8,4},{12,8},{16,12},{20,16},{24,20},{28,24},{5,1},{9,5},{13... | collective-permute-start | bytes 202760 | tf_op jit(solution)/shard_map/while/body/eval_jaxpr/ppermute | solution.py:23
  162.2 10.5 %collective-permute-start.3 = (f32[4,2,16,132]{3,2,1,0:T(8,128)S(1)}, f32[4,2,16,132]{3,2,1,0:T(8,128)S(1)}, u32[]{:S(2)}, u32[]{:S(2)}) collective-permute-start(f32[4,2,16,132]{3,2,1,0:T(8,128)S(1)} %get-tuple-element.311), channel_id=1, source_target_pairs={{0,4},{4,8},{8,12},{12,16},{16,20},{20,24},{24,28},{1,5},{5,9},{9,... | collective-permute-start | bytes 202760 | tf_op jit(solution)/shard_map/while/body/eval_jaxpr/ppermute | solution.py:22
  184.7 7.3 %collective-permute-start = (f32[4,4,16,2]{3,2,1,0:T(8,128)S(1)}, f32[4,4,16,2]{3,2,1,0:T(8,128)S(1)}, u32[]{:S(2)}, u32[]{:S(2)}) collective-permute-start(f32[4,4,16,2]{3,2,1,0:T(8,128)S(1)} %get-tuple-element.308), channel_id=1, source_target_pairs={{32,0},{64,32},{96,64},{33,1},{65,33},{97,65},{34,2},{66,34},{98,6... | collective-permute-start | bytes 6152 | tf_op jit(solution)/shard_map/while/body/eval_jaxpr/ppermute | solution.py:23
  186.0 7.5 %collective-permute-start.1 = (f32[4,4,16,2]{3,2,1,0:T(8,128)S(1)}, f32[4,4,16,2]{3,2,1,0:T(8,128)S(1)}, u32[]{:S(2)}, u32[]{:S(2)}) collective-permute-start(f32[4,4,16,2]{3,2,1,0:T(8,128)S(1)} %get-tuple-element.309), channel_id=1, source_target_pairs={{0,32},{32,64},{64,96},{1,33},{33,65},{65,97},{2,34},{34,66},{66,9... | collective-permute-start | bytes 6152 | tf_op jit(solution)/shard_map/while/body/eval_jaxpr/ppermute | solution.py:22
  194.4 7.1 %collective-permute-start.2 = (f32[4,2,16,132]{3,2,1,0:T(8,128)}, f32[4,2,16,132]{3,2,1,0:T(8,128)S(1)}, u32[]{:S(2)}, u32[]{:S(2)}) collective-permute-start(f32[4,2,16,132]{3,2,1,0:T(8,128)} %get-tuple-element.310), channel_id=1, source_target_pairs={{4,0},{8,4},{12,8},{16,12},{20,16},{24,20},{28,24},{5,1},{9,5},{13... | collective-permute-start | bytes 202760 | tf_op jit(solution)/shard_map/while/body/eval_jaxpr/ppermute | solution.py:23
  196.3 10.5 %collective-permute-start.3 = (f32[4,2,16,132]{3,2,1,0:T(8,128)S(1)}, f32[4,2,16,132]{3,2,1,0:T(8,128)S(1)}, u32[]{:S(2)}, u32[]{:S(2)}) collective-permute-start(f32[4,2,16,132]{3,2,1,0:T(8,128)S(1)} %get-tuple-element.311), channel_id=1, source_target_pairs={{0,4},{4,8},{8,12},{12,16},{16,20},{20,24},{24,28},{1,5},{5,9},{9,... | collective-permute-start | bytes 202760 | tf_op jit(solution)/shard_map/while/body/eval_jaxpr/ppermute | solution.py:22
  218.9 7.3 %collective-permute-start = (f32[4,4,16,2]{3,2,1,0:T(8,128)S(1)}, f32[4,4,16,2]{3,2,1,0:T(8,128)S(1)}, u32[]{:S(2)}, u32[]{:S(2)}) collective-permute-start(f32[4,4,16,2]{3,2,1,0:T(8,128)S(1)} %get-tuple-element.308), channel_id=1, source_target_pairs={{32,0},{64,32},{96,64},{33,1},{65,33},{97,65},{34,2},{66,34},{98,6... | collective-permute-start | bytes 6152 | tf_op jit(solution)/shard_map/while/body/eval_jaxpr/ppermute | solution.py:23
  220.2 7.5 %collective-permute-start.1 = (f32[4,4,16,2]{3,2,1,0:T(8,128)S(1)}, f32[4,4,16,2]{3,2,1,0:T(8,128)S(1)}, u32[]{:S(2)}, u32[]{:S(2)}) collective-permute-start(f32[4,4,16,2]{3,2,1,0:T(8,128)S(1)} %get-tuple-element.309), channel_id=1, source_target_pairs={{0,32},{32,64},{64,96},{1,33},{33,65},{65,97},{2,34},{34,66},{66,9... | collective-permute-start | bytes 6152 | tf_op jit(solution)/shard_map/while/body/eval_jaxpr/ppermute | solution.py:22
  228.5 7.1 %collective-permute-start.2 = (f32[4,2,16,132]{3,2,1,0:T(8,128)}, f32[4,2,16,132]{3,2,1,0:T(8,128)S(1)}, u32[]{:S(2)}, u32[]{:S(2)}) collective-permute-start(f32[4,2,16,132]{3,2,1,0:T(8,128)} %get-tuple-element.310), channel_id=1, source_target_pairs={{4,0},{8,4},{12,8},{16,12},{20,16},{24,20},{28,24},{5,1},{9,5},{13... | collective-permute-start | bytes 202760 | tf_op jit(solution)/shard_map/while/body/eval_jaxpr/ppermute | solution.py:23
  230.4 10.5 %collective-permute-start.3 = (f32[4,2,16,132]{3,2,1,0:T(8,128)S(1)}, f32[4,2,16,132]{3,2,1,0:T(8,128)S(1)}, u32[]{:S(2)}, u32[]{:S(2)}) collective-permute-start(f32[4,2,16,132]{3,2,1,0:T(8,128)S(1)} %get-tuple-element.311), channel_id=1, source_target_pairs={{0,4},{4,8},{8,12},{12,16},{16,20},{20,24},{24,28},{1,5},{5,9},{9,... | collective-permute-start | bytes 202760 | tf_op jit(solution)/shard_map/while/body/eval_jaxpr/ppermute | solution.py:22
  253.0 7.3 %collective-permute-start = (f32[4,4,16,2]{3,2,1,0:T(8,128)S(1)}, f32[4,4,16,2]{3,2,1,0:T(8,128)S(1)}, u32[]{:S(2)}, u32[]{:S(2)}) collective-permute-start(f32[4,4,16,2]{3,2,1,0:T(8,128)S(1)} %get-tuple-element.308), channel_id=1, source_target_pairs={{32,0},{64,32},{96,64},{33,1},{65,33},{97,65},{34,2},{66,34},{98,6... | collective-permute-start | bytes 6152 | tf_op jit(solution)/shard_map/while/body/eval_jaxpr/ppermute | solution.py:23
  254.3 7.5 %collective-permute-start.1 = (f32[4,4,16,2]{3,2,1,0:T(8,128)S(1)}, f32[4,4,16,2]{3,2,1,0:T(8,128)S(1)}, u32[]{:S(2)}, u32[]{:S(2)}) collective-permute-start(f32[4,4,16,2]{3,2,1,0:T(8,128)S(1)} %get-tuple-element.309), channel_id=1, source_target_pairs={{0,32},{32,64},{64,96},{1,33},{33,65},{65,97},{2,34},{34,66},{66,9... | collective-permute-start | bytes 6152 | tf_op jit(solution)/shard_map/while/body/eval_jaxpr/ppermute | solution.py:22
  262.6 7.1 %collective-permute-start.2 = (f32[4,2,16,132]{3,2,1,0:T(8,128)}, f32[4,2,16,132]{3,2,1,0:T(8,128)S(1)}, u32[]{:S(2)}, u32[]{:S(2)}) collective-permute-start(f32[4,2,16,132]{3,2,1,0:T(8,128)} %get-tuple-element.310), channel_id=1, source_target_pairs={{4,0},{8,4},{12,8},{16,12},{20,16},{24,20},{28,24},{5,1},{9,5},{13... | collective-permute-start | bytes 202760 | tf_op jit(solution)/shard_map/while/body/eval_jaxpr/ppermute | solution.py:23
  264.6 10.5 %collective-permute-start.3 = (f32[4,2,16,132]{3,2,1,0:T(8,128)S(1)}, f32[4,2,16,132]{3,2,1,0:T(8,128)S(1)}, u32[]{:S(2)}, u32[]{:S(2)}) collective-permute-start(f32[4,2,16,132]{3,2,1,0:T(8,128)S(1)} %get-tuple-element.311), channel_id=1, source_target_pairs={{0,4},{4,8},{8,12},{12,16},{16,20},{20,24},{24,28},{1,5},{5,9},{9,... | collective-permute-start | bytes 202760 | tf_op jit(solution)/shard_map/while/body/eval_jaxpr/ppermute | solution.py:22
  287.1 7.3 %collective-permute-start = (f32[4,4,16,2]{3,2,1,0:T(8,128)S(1)}, f32[4,4,16,2]{3,2,1,0:T(8,128)S(1)}, u32[]{:S(2)}, u32[]{:S(2)}) collective-permute-start(f32[4,4,16,2]{3,2,1,0:T(8,128)S(1)} %get-tuple-element.308), channel_id=1, source_target_pairs={{32,0},{64,32},{96,64},{33,1},{65,33},{97,65},{34,2},{66,34},{98,6... | collective-permute-start | bytes 6152 | tf_op jit(solution)/shard_map/while/body/eval_jaxpr/ppermute | solution.py:23
  288.4 7.5 %collective-permute-start.1 = (f32[4,4,16,2]{3,2,1,0:T(8,128)S(1)}, f32[4,4,16,2]{3,2,1,0:T(8,128)S(1)}, u32[]{:S(2)}, u32[]{:S(2)}) collective-permute-start(f32[4,4,16,2]{3,2,1,0:T(8,128)S(1)} %get-tuple-element.309), channel_id=1, source_target_pairs={{0,32},{32,64},{64,96},{1,33},{33,65},{65,97},{2,34},{34,66},{66,9... | collective-permute-start | bytes 6152 | tf_op jit(solution)/shard_map/while/body/eval_jaxpr/ppermute | solution.py:22
  296.8 7.1 %collective-permute-start.2 = (f32[4,2,16,132]{3,2,1,0:T(8,128)}, f32[4,2,16,132]{3,2,1,0:T(8,128)S(1)}, u32[]{:S(2)}, u32[]{:S(2)}) collective-permute-start(f32[4,2,16,132]{3,2,1,0:T(8,128)} %get-tuple-element.310), channel_id=1, source_target_pairs={{4,0},{8,4},{12,8},{16,12},{20,16},{24,20},{28,24},{5,1},{9,5},{13... | collective-permute-start | bytes 202760 | tf_op jit(solution)/shard_map/while/body/eval_jaxpr/ppermute | solution.py:23
  298.7 10.5 %collective-permute-start.3 = (f32[4,2,16,132]{3,2,1,0:T(8,128)S(1)}, f32[4,2,16,132]{3,2,1,0:T(8,128)S(1)}, u32[]{:S(2)}, u32[]{:S(2)}) collective-permute-start(f32[4,2,16,132]{3,2,1,0:T(8,128)S(1)} %get-tuple-element.311), channel_id=1, source_target_pairs={{0,4},{4,8},{8,12},{12,16},{16,20},{20,24},{24,28},{1,5},{5,9},{9,... | collective-permute-start | bytes 202760 | tf_op jit(solution)/shard_map/while/body/eval_jaxpr/ppermute | solution.py:22
  (51 other events, 189.9 us)
where the time goes:
time: 436 us; the launch traced here: 433 us
  starting transfers between devices  155 us (36%)
  waiting for transfers between devices  107 us (25%)
  blocking collectives  82.8 us (19%)
  other arithmetic  39 us (9%)
  matrix products  26.3 us (6%)
  local copies, waits for them, and re-layouts  21.4 us (5%)
    ppermute x27, starting transfers between devices, padded_2(): before = lax.ppermute(last, axis, up)  97.3 us
    ppermute x27, waiting for transfers between devices, padded_2(): before = lax.ppermute(last, axis, up)  82.5 us
    psum x10, blocking collectives, by_axis(): return functools.reduce(lax.psum, axes, value)  63.3 us
    ppermute x27, starting transfers between devices, padded_2(): after = lax.ppermute(leading, axis, down)  57.5 us
    ppermute x27, waiting for transfers between devices, padded_2(): after = lax.ppermute(leading, axis, down)  24.1 us
    all_to_all x1, blocking collectives, body(): lax.all_to_all(snaps, 'grp', split_axis=1, concat_axis=4, tiled=True)  19.4 us
    dot_general x1, matrix products, body(): jnp.dot(rest.astype(jnp.bfloat16), local, preferred_element_type=jnp.floa...  17 us
    mul x8, other arithmetic, pair_step(): middle = advance(padded, diffusion, rim[0], rim[2:]) * rim[1][None]  9.94 us
  transfers between devices with their start and end apart: 54, of which 45 were waited for; matrix products, arithmetic and copies ran while one was open for 2% of the time, Pallas kernels for 0%

commit v1 on v0

v1 whole, which is shorter than its diff:
```python
import jax
import jax.numpy as jnp
from jax import lax
from jax.experimental import pallas as pl
from jax.experimental.pallas import tpu as pltpu
from jax.sharding import PartitionSpec as P

SPEC = 4
MATS = 8
STEPS = 16
ROUNDS = STEPS // 2
SNAPS = 8
MODES = 256
CX, CY, CZ = 4, 16, 128
ROWS = CX * CY
BASIS_ROWS = ROWS * 512
PART = BASIS_ROWS // ROUNDS
MESH = pl.DeviceIdType.MESH
F32 = jnp.float32
BF16 = jnp.bfloat16

FACES = [(-1, 0, 0), (1, 0, 0), (0, -1, 0), (0, 1, 0), (0, 0, -1), (0, 0, 1)]
XZ = [(a, 0, b) for a in (-1, 1) for b in (-1, 1)]
XY = [(a, b, 0) for a in (-1, 1) for b in (-1, 1)]
YZ = [(0, a, b) for a in (-1, 1) for b in (-1, 1)]
DIRS = FACES + XZ + XY + YZ
ORDER = [0, 1, 6, 7, 8, 9, 10, 11, 12, 13, 4, 5, 14, 15, 16, 17, 2, 3]


def kernel(
    terminal, diffusion, velocity, material, rates, stoich, plan, basis,
    coeff_out, adj_out,
    bv, st, fields, rx, ry, rz, pack, edge, cx, cy, cz, lam, mid,
    kc, vm, dm, rc, gram, got, proj, suma, sumb,
    basis_sem, hs, hr, cs, cr, as_, ar, ss, sr,
):
    g = lax.axis_index("grp")
    x = lax.axis_index("gx")
    y = lax.axis_index("gy")
    n_g, n_x, n_y = 4, 8, 4

    def has(d):
        cond = None
        for step, at, count in ((d[0], x, n_x), (d[1], y, n_y), (d[2], g, n_g)):
            if step == 0:
                continue
            term = at > 0 if step < 0 else at < count - 1
            cond = term if cond is None else jnp.logical_and(cond, term)
        return cond

    def minus(d):
        return tuple(-v for v in d)

    def dev(d):
        return (g + d[2], x + d[0], y + d[1])

    sub = lax.broadcasted_iota(jnp.int32, (8, CZ), 0)
    lane = lax.broadcasted_iota(jnp.int32, (8, CZ), 1)
    odd_lane = lax.rem(lane, 2) == 1
    odd_sub = lax.rem(sub, 2) == 1

    def low(cond, most):
        return jnp.where(cond, most, 0)

    def high(cond, least, size):
        return jnp.where(cond, least, size)

    def basis_copy(c):
        rows = pl.ds(c * PART, PART)
        return pltpu.make_async_copy(basis.at[rows, :], bv.at[rows, :], basis_sem.at[c])

    for c in range(ROUNDS):
        basis_copy(c).start()

    st[0] = terminal[...]
    fields[0] = velocity[...]
    fields[1] = material[...].astype(F32)
    lam[...] = jnp.zeros_like(lam)

    barrier = pltpu.get_barrier_semaphore()
    ga = g * n_y + y

    def group_a(o):
        q = lax.rem(ga + o, n_g * n_y)
        return q, (q // n_y, x, lax.rem(q, n_y))

    def group_b(o):
        q = lax.rem(x + o, n_x)
        return q, (g, q, y)

    count = jnp.int32(n_g * n_y - 1 + n_x - 1)
    for o in range(1, n_g * n_y):
        pl.semaphore_signal(barrier, inc=1, device_id=group_a(o)[1], device_id_type=MESH)
    for o in range(1, n_x):
        pl.semaphore_signal(barrier, inc=1, device_id=group_b(o)[1], device_id_type=MESH)
    for d in XZ + XY:
        cond = has(d)
        count = count + cond.astype(jnp.int32)

        @pl.when(cond)
        def _(d=d):
            pl.semaphore_signal(barrier, inc=1, device_id=dev(d), device_id_type=MESH)

    pl.semaphore_wait(barrier, count)

    def halo_copy(i, k, par):
        d = DIRS[i]
        n = 2 * k
        if i < 2:
            src = st.at[n, :, pl.ds(0 if i == 0 else 2, 2)]
            dst = rx.at[par, i]
        elif i < 4:
            src = st.at[n, :, :, pl.ds(0 if i == 2 else 8, 8), :]
            dst = ry.at[par, i - 2]
        elif i < 6:
            src = st.at[n]
            dst = rz.at[par, i - 4]
        else:
            if i < 10:
                which = (i - 6) // 2
            elif i < 14:
                which = 2 + (i - 10) // 2
            else:
                which = 4
            src = pack.at[par, which]
            dst = edge.at[par, i - 6]
        return pltpu.make_async_remote_copy(
            src_ref=src, dst_ref=dst, send_sem=hs.at[par, i], recv_sem=hr.at[par, i],
            device_id=dev(d), device_id_type=MESH,
        )

    def pack_edges(k, par):
        n = 2 * k
        for side in (0, 1):
            plane = 0 if side == 0 else CX - 1
            acc = jnp.zeros((8, CZ), F32)
            rows = jnp.zeros((8, CZ), F32)
            for s in range(SPEC):
                t0 = st[n, s, plane, 0:8, :]
                t1 = st[n, s, plane, 8:16, :]
                for t, v in ((0, t0), (1, t1)):
                    i = 2 * (s * 2 + t)
                    hit = jnp.logical_or(lane == i, lane == (i - 1) % CZ)
                    acc = jnp.where(hit, pltpu.roll(v, i, 1) if i else v, acc)
                i = 2 * s
                both = jnp.where(sub < 4, t0, t1)
                hit = jnp.logical_or(sub == i, sub == (i - 1) % 8)
                rows = jnp.where(hit, pltpu.roll(both, i, 0) if i else both, rows)
            pack[par, side] = acc
            pack[par, 2 + side] = rows
        acc = jnp.zeros((8, CZ), F32)
        for s in range(SPEC):
            for p in range(CX):
                i = 2 * (s * CX + p)
                v = jnp.where(sub < 4, st[n, s, p, 0:8, :], st[n, s, p, 8:16, :])
                hit = jnp.logical_or(lane == i, lane == (i - 1) % CZ)
                acc = jnp.where(hit, pltpu.roll(v, i, 1) if i else v, acc)
        pack[par, 4] = acc

    def start_halo(k, par):
        pack_edges(k, par)
        for i in ORDER:

            @pl.when(has(DIRS[i]))
            def _(i=i):
                halo_copy(i, k, par).start()

    def wait_halo(k, par):
        for i in ORDER:

            @pl.when(has(minus(DIRS[i])))
            def _(i=i):
                halo_copy(i, k, par).wait_recv()

    def wait_sent(k, par):
        for i in ORDER:

            @pl.when(has(DIRS[i]))
            def _(i=i):
                halo_copy(i, k, par).wait_send()

    xm, xp = has((-1, 0, 0)), has((1, 0, 0))
    ym, yp = has((0, -1, 0)), has((0, 1, 0))
    zm, zp = has((0, 0, -1)), has((0, 0, 1))
    y_from_p = sub < low(yp, 4)
    y_from_m = sub >= high(ym, 4, 8)
    lane_full = lax.broadcasted_iota(jnp.int32, (CY, CZ), 1)
    z_from_p = lane_full < low(zp, 64)
    z_from_m = lane_full >= high(zm, 64, CZ)

    def unpack(par):
        zero8 = jnp.zeros((8, CZ), F32)
        for s in range(SPEC):
            lam[s, 0:2, 0:16, 0:128] = jnp.where(xm, rx[par, 1, s], 0.0)
            lam[s, 6:8, 0:16, 0:128] = jnp.where(xp, rx[par, 0, s], 0.0)
            for p in range(CX):
                lam[s, 2 + p, 16:24, 0:128] = jnp.where(
                    y_from_p, ry[par, 0, s, p], jnp.where(y_from_m, ry[par, 1, s, p], zero8))
                lam[s, 2 + p, 0:16, 128:256] = jnp.where(
                    z_from_p, rz[par, 0, s, p], jnp.where(z_from_m, rz[par, 1, s, p], 0.0))

        def flag(a, b):
            return jnp.logical_and(a, b)

        for side, xh in ((1, xm), (0, xp)):
            base = side * 2
            m_m, m_p = edge[par, base + 1], edge[par, base]
            comb = jnp.where(
                jnp.logical_and(odd_lane, lane < low(flag(xh, zm), CZ)), m_m,
                jnp.where(
                    jnp.logical_and(jnp.logical_not(odd_lane), lane < low(flag(xh, zp), CZ)),
                    m_p, zero8))
            at = 1 if side == 1 else 6
            for s in range(SPEC):
                for t in range(2):
                    i = 2 * (s * 2 + t)
                    tile = pltpu.roll(comb, (CZ - i) % CZ, 1) if i else comb
                    lam[s, at, t * 8:(t + 1) * 8, 128:256] = tile
        for side, xh in ((1, xm), (0, xp)):
            base = 4 + side * 2
            m_m, m_p = edge[par, base + 1], edge[par, base]
            comb = jnp.where(
                jnp.logical_and(odd_sub, sub < low(flag(xh, ym), 8)), m_m,
                jnp.where(
                    jnp.logical_and(jnp.logical_not(odd_sub), sub < low(flag(xh, yp), 8)),
                    m_p, zero8))
            at = 1 if side == 1 else 6
            for s in range(SPEC):
                i = 2 * s
                tile = pltpu.roll(comb, (8 - i) % 8, 0) if i else comb
                lam[s, at, 16:24, 0:128] = tile
        even_lane = jnp.logical_not(odd_lane)
        hi_m = jnp.logical_and(odd_lane, sub >= high(flag(ym, zm), 4, 8))
        hi_p = jnp.logical_and(even_lane, sub >= high(flag(ym, zp), 4, 8))
        lo_m = jnp.logical_and(odd_lane, sub < low(flag(yp, zm), 4))
        lo_p = jnp.logical_and(even_lane, sub < low(flag(yp, zp), 4))
        comb = jnp.where(hi_m, edge[par, 11], zero8)
        comb = jnp.where(hi_p, edge[par, 10], comb)
        comb = jnp.where(lo_m, edge[par, 9], comb)
        comb = jnp.where(lo_p, edge[par, 8], comb)
        for s in range(SPEC):
            for p in range(CX):
                i = 2 * (s * CX + p)
                tile = pltpu.roll(comb, (CZ - i) % CZ, 1) if i else comb
                lam[s, 2 + p, 16:24, 128:256] = tile

    def coeff_copy(i):
        if i < 2:
            src = fields.at[:, pl.ds(0 if i == 0 else CX - 1, 1)]
            dst = cx.at[i]
        elif i < 4:
            src = fields.at[:, :, pl.ds(0 if i == 2 else 8, 8), :]
            dst = cy.at[i - 2]
        else:
            src = fields
            dst = cz.at[i - 4]
        return pltpu.make_async_remote_copy(
            src_ref=src, dst_ref=dst, send_sem=cs.at[i], recv_sem=cr.at[i],
            device_id=dev(DIRS[i]), device_id_type=MESH,
        )

    for i in range(6):

        @pl.when(has(DIRS[i]))
        def _(i=i):
            coeff_copy(i).start()

    def snap_copy(k, o):
        q = lax.rem(g + o, n_g)
        return pltpu.make_async_remote_copy(
            src_ref=st.at[pl.ds(2 * k + 1, 2), q],
            dst_ref=got.at[pl.ds(2 * k, 2), g],
            send_sem=as_.at[k, o - 1], recv_sem=ar.at[k, o - 1],
            device_id=(q, x, y), device_id_type=MESH,
        )

    gram[...] = jnp.zeros_like(gram)
    lam[:, 2:6, 0:16, 0:128] = terminal[...]

    def coefficients():
        sub24 = lax.broadcasted_iota(jnp.int32, (24, 256), 0)
        lane24 = lax.broadcasted_iota(jnp.int32, (24, 256), 1)
        for p in range(6):
            own = 1 <= p <= CX
            for r0, r1, l0, l1 in ((0, 16, 0, 128), (16, 24, 0, 128), (0, 16, 128, 256)):
                if not own and (r0, l0) != (0, 0):
                    continue
                vals = []
                for f in range(2):
                    if not own:
                        side, ok = (1, xm) if p == 0 else (0, xp)
                        v = jnp.where(ok, cx[side, f, 0], 0.0)
                    elif (r0, l0) == (0, 0):
                        v = fields[f, p - 1]
                    elif r0 == 16:
                        v = jnp.where(y_from_p, cy[0, f, p - 1],
                                      jnp.where(y_from_m, cy[1, f, p - 1], 0.0))
                    else:
                        v = jnp.where(z_from_p, cz[0, f, p - 1],
                                      jnp.where(z_from_m, cz[1, f, p - 1], 0.0))
                    vals.append(v)
                vel, mat = vals
                if not own:
                    ok = xm if p == 0 else xp
                    inside = jnp.where(ok, 1.0, 0.0) * jnp.ones((16, 128), F32)
                elif (r0, l0) == (0, 0):
                    inside = jnp.ones((16, 128), F32)
                elif r0 == 16:
                    inside = jnp.where(jnp.logical_or(y_from_p, y_from_m), 1.0, 0.0)
                else:
                    inside = jnp.where(jnp.logical_or(z_from_p, z_from_m), 1.0, 0.0)
                looked = []
                for r in range(8):
                    v = jnp.full(mat.shape, rates[0, r], F32)
                    for m in range(1, MATS):
                        v = jnp.where(mat == float(m), rates[m, r], v)
                    looked.append(v * inside)
                vel = vel * inside
                vm[p, r0:r1, l0:l1] = vel
                for a in range(SPEC):
                    dm[a, p, r0:r1, l0:l1] = inside * diffusion[a]
                    for b in range(SPEC):
                        v = (looked[a] * stoich[a, b].astype(F32)
                             + looked[a + 4] * stoich[a + 4, b].astype(F32))
                        if a == b:
                            kc[a, p, r0:r1, l0:l1] = (
                                inside * (1.0 - 6.0 * diffusion[a]) - vel + v)
                        else:
                            rc[a, b, p, r0:r1, l0:l1] = v

    def advance(cs_, s, p, tile, dn, up, ys, zs):
        r0, r1, l0, l1 = tile
        box = (p, slice(r0, r1), slice(l0, l1))
        total = dm[(s,) + box] * (((dn + up) + ys) + zs)
        total = total + kc[(s,) + box] * cs_[s]
        total = total + vm[box] * up
        for b in range(SPEC):
            if b != s:
                total = total + rc[(s, b) + box] * cs_[b]
        return total

    own_tile = (0, 16, 0, 128)

    def first_step():
        for p in range(6):
            full = [lam[s, p + 1] for s in range(SPEC)]
            for s in range(SPEC):
                c = full[s]
                ya = pltpu.roll(c, 1, 0) + pltpu.roll(c, 23, 0)
                za = pltpu.roll(c, 1, 1) + pltpu.roll(c, 255, 1)
                tiles = [own_tile]
                if 1 <= p <= CX:
                    tiles += [(16, 24, 0, 128), (0, 16, 128, 256)]
                for t in tiles:
                    r0, r1, l0, l1 = t
                    mid[s, p, r0:r1, l0:l1] = advance(
                        [v[r0:r1, l0:l1] for v in full], s, p, t,
                        lam[s, p, r0:r1, l0:l1], lam[s, p + 2, r0:r1, l0:l1],
                        ya[r0:r1, l0:l1], za[r0:r1, l0:l1])

    def second_step(n):
        for p in range(1, 1 + CX):
            own = [mid[s, p, 0:16, 0:128] for s in range(SPEC)]
            for s in range(SPEC):
                col = mid[s, p, :, 0:128]
                ya = (pltpu.roll(col, 1, 0) + pltpu.roll(col, 23, 0))[0:16]
                row = mid[s, p, 0:16, :]
                za = (pltpu.roll(row, 1, 1) + pltpu.roll(row, 255, 1))[:, 0:128]
                new = advance(own, s, p, own_tile, mid[s, p - 1, 0:16, 0:128],
                              mid[s, p + 1, 0:16, 0:128], ya, za)
                st[n + 1, s, p - 1] = own[s]
                st[n + 2, s, p - 1] = new
                lam[s, p + 1, 0:16, 0:128] = new

    mid[...] = jnp.zeros_like(mid)

    def gram_part(k):
        rows = 512

        def one(c, carry):
            at = pl.multiple_of(k * PART + c * rows, rows)
            block = bv[pl.ds(at, rows), :]
            gram[...] += lax.dot_general(
                block, block, (((0,), (0,)), ((), ())), preferred_element_type=F32)
            return carry

        lax.fori_loop(0, PART // rows, one, 0)

    start_halo(0, 0)
    for i in range(6):

        @pl.when(has(minus(DIRS[i])))
        def _(i=i):
            coeff_copy(i).wait_recv()

    coefficients()

    def round_(k, carry):
        par = lax.rem(k, 2)

        @pl.when(k > 0)
        def _():
            start_halo(k, par)
            for o in range(1, n_g):
                snap_copy(k - 1, o).start()

        basis_copy(k).wait()
        gram_part(k)
        wait_halo(k, par)
        unpack(par)
        first_step()
        second_step(2 * k)
        wait_sent(k, par)
        got[pl.ds(2 * k, 2), g] = st[pl.ds(2 * k + 1, 2), g]
        return carry

    lax.fori_loop(0, ROUNDS, round_, 0)
    for o in range(1, n_g):
        snap_copy(ROUNDS - 1, o).start()
    adj_out[...] = st[STEPS]
    for i in range(6):

        @pl.when(has(DIRS[i]))
        def _(i=i):
            coeff_copy(i).wait_send()

    def snap_wait(k, carry):
        for o in range(1, n_g):
            snap_copy(k, o).wait_recv()
        return carry

    lax.fori_loop(0, ROUNDS, snap_wait, 0)

    flat = got.reshape(STEPS * 4 * ROWS, CZ)
    proj[...] = jnp.zeros_like(proj)

    def project(c, carry):
        total = jnp.zeros((2 * STEPS, MODES), F32)
        for u in range(4):
            at = c * 4 + u
            vals = [flat[pl.ds(zq * ROWS + at, STEPS, stride=4 * ROWS), :] for zq in range(4)]
            a = jnp.concatenate(vals, axis=1)
            hi = a.astype(BF16)
            lo = (a - hi.astype(F32)).astype(BF16)
            both = jnp.concatenate([hi, lo], axis=0)
            rows = pl.ds(pl.multiple_of(at * 512, 512), 512)
            total += jnp.dot(both, bv[rows, :], preferred_element_type=F32)
        proj[...] += total
        return carry

    lax.fori_loop(0, ROWS // 4, project, 0)

    slot = lax.broadcasted_iota(jnp.int32, (SNAPS, MODES), 0)
    step_of = jnp.zeros((SNAPS, MODES), jnp.int32)
    for j in range(SNAPS):
        step_of = jnp.where(slot == j, plan[j], step_of)
    first = jnp.zeros((SNAPS, MODES), F32)
    rest = jnp.zeros((SNAPS, MODES), F32)
    for n in range(STEPS):
        hit = step_of == n
        first = jnp.where(hit, jnp.broadcast_to(proj[n:n + 1, :], first.shape), first)
        rest = jnp.where(
            hit, jnp.broadcast_to(proj[STEPS + n:STEPS + n + 1, :], first.shape), rest)

    def all_sum(value, turn):
        suma[turn, ga] = value

        def a_copy(o):
            q, where = group_a(o)
            return pltpu.make_async_remote_copy(
                src_ref=suma.at[turn, ga], dst_ref=suma.at[turn, ga],
                send_sem=ss.at[turn, 0, o], recv_sem=sr.at[turn, 0, o],
                device_id=where, device_id_type=MESH)

        def b_copy(o):
            q, where = group_b(o)
            return pltpu.make_async_remote_copy(
                src_ref=sumb.at[turn, x], dst_ref=sumb.at[turn, x],
                send_sem=ss.at[turn, 1, o], recv_sem=sr.at[turn, 1, o],
                device_id=where, device_id_type=MESH)

        for o in range(1, n_g * n_y):
            a_copy(o).start()
        for o in range(1, n_g * n_y):
            a_copy(o).wait_recv()
        total = suma[turn, 0]
        for q in range(1, n_g * n_y):
            total = total + suma[turn, q]
        sumb[turn, x] = total
        for o in range(1, n_x):
            b_copy(o).start()
        for o in range(1, n_x):
            b_copy(o).wait_recv()
        total = sumb[turn, 0]
        for q in range(1, n_x):
            total = total + sumb[turn, q]

        def finish():
            for o in range(1, n_g * n_y):
                a_copy(o).wait_send()
            for o in range(1, n_x):
                b_copy(o).wait_send()

        return total, finish

    total, finish_0 = all_sum(first, 0)
    low_first = total.astype(BF16)
    gm = gram[...]
    g1 = gm.astype(BF16)
    left = gm - g1.astype(F32)
    g2 = left.astype(BF16)
    g3 = (left - g2.astype(F32)).astype(BF16)
    back = jnp.dot(low_first, g1, preferred_element_type=F32)
    back += jnp.dot(low_first, g2, preferred_element_type=F32)
    back += jnp.dot(low_first, g3, preferred_element_type=F32)
    second = (first - back) + rest
    more, finish_1 = all_sum(second, 1)
    coeff_out[...] = total + more
    finish_0()
    finish_1()

    def snap_sent(k, carry):
        for o in range(1, n_g):
            snap_copy(k, o).wait_send()
        return carry

    lax.fori_loop(0, ROUNDS, snap_sent, 0)


def body(terminal, diffusion, velocity, material, rates, stoich, plan, basis):
    vmem = pl.BlockSpec(memory_space=pltpu.VMEM)
    smem = pl.BlockSpec(memory_space=pltpu.SMEM)
    dma = pltpu.SemaphoreType.DMA
    v = pltpu.VMEM
    return pl.pallas_call(
        kernel,
        out_shape=(
            jax.ShapeDtypeStruct((SNAPS, MODES), F32),
            jax.ShapeDtypeStruct((SPEC, CX, CY, CZ), F32),
        ),
        in_specs=[vmem, smem, vmem, vmem, smem, smem, smem, pl.BlockSpec(memory_space=pl.ANY)],
        out_specs=(vmem, vmem),
        scratch_shapes=[
            v((BASIS_ROWS, MODES), BF16),
            v((STEPS + 1, SPEC, CX, CY, CZ), F32),
            v((2, CX, CY, CZ), F32),
            v((2, 2, SPEC, 2, CY, CZ), F32),
            v((2, 2, SPEC, CX, 8, CZ), F32),
            v((2, 2, SPEC, CX, CY, CZ), F32),
            v((2, 5, 8, CZ), F32),
            v((2, 12, 8, CZ), F32),
            v((2, 2, 1, CY, CZ), F32),
            v((2, 2, CX, 8, CZ), F32),
            v((2, 2, CX, CY, CZ), F32),
            v((SPEC, 8, 24, 256), F32),
            v((SPEC, 6, 24, 256), F32),
            v((SPEC, 6, 24, 256), F32),
            v((6, 24, 256), F32),
            v((SPEC, 6, 24, 256), F32),
            v((SPEC, SPEC, 6, 24, 256), F32),
            v((MODES, MODES), F32),
            v((STEPS, 4, CX, CY, CZ), F32),
            v((2 * STEPS, MODES), F32),
            v((2, 16, SNAPS, MODES), F32),
            v((2, 8, SNAPS, MODES), F32),
            dma((ROUNDS,)),
            dma((2, 18)),
            dma((2, 18)),
            dma((6,)),
            dma((6,)),
            dma((ROUNDS, 3)),
            dma((ROUNDS, 3)),
            dma((2, 2, 16)),
            dma((2, 2, 16)),
        ],
        compiler_params=pltpu.CompilerParams(
            collective_id=0, has_side_effects=True, vmem_limit_bytes=60 * 1024 * 1024
        ),
    )(
        terminal, diffusion, velocity, material, rates, stoich, plan,
        basis.reshape(BASIS_ROWS, MODES),
    )


def solution(mesh):
    return jax.shard_map(
        body,
        mesh=mesh,
        in_specs=(
            P(None, "gx", "gy", "grp"),
            P(),
            P("gx", "gy", "grp"),
            P("gx", "gy", "grp"),
            P(),
            P(),
            P(),
            P("grp", "gx", "gy", None, None),
        ),
        out_specs=(P(), P(None, "gx", "gy", "grp")),
        check_vma=False,
    )
```

time: 436 us -> 104 us (0.24)
  starting transfers between devices: 155 us -> 0 us
  waiting for transfers between devices: 107 us -> 0 us
  Pallas kernels: 0 us -> 97.5 us
  blocking collectives: 82.8 us -> 0 us
  other arithmetic: 39 us -> 0 us
  matrix products: 26.3 us -> 0 us
  local copies, waits for them, and re-layouts: 21.4 us -> 4.21 us
    ppermute x54 -> x0, starting transfers between devices: 155 us -> none  [the longest x27 97.3 us: padded_2(): before = lax.ppermute(last, axis, up)]
    ppermute x54 -> x0, waiting for transfers between devices: 107 us -> none  [the longest x27 82.5 us: padded_2(): before = lax.ppermute(last, axis, up)]
    pallas_call x0 -> x1, Pallas kernels: none -> 97.5 us  [body(): pl.pallas_call(kernel, out_shape=(jax.ShapeDtypeStruct((SNAPS, MODES), F3...]
    psum x10 -> x0, blocking collectives: 63.3 us -> none  [by_axis(): return functools.reduce(lax.psum, axes, value)]
    dot_general x4 -> x0, matrix products: 26.3 us -> none  [the longest x1 17 us: body(): jnp.dot(rest.astype(jnp.bfloat16), local, preferred_element_type=jnp.floa...]
    all_to_all x1 -> x0, blocking collectives: 19.4 us -> none  [body(): lax.all_to_all(snaps, 'grp', split_axis=1, concat_axis=4, tiled=True)]
    mul x16 -> x0, other arithmetic: 11.8 us -> none  [the longest x8 9.94 us: pair_step(): middle = advance(padded, diffusion, rim[0], rim[2:]) * rim[1][None]]
    slice x18 -> x0, other arithmetic: 9.98 us -> none  [the longest x10 7.7 us: padded_2(): last = lax.slice_in_dim(value, length - width, length, axis=dim)]
  transfers between devices with their start and end apart: 54 -> 0, of which waited for: 45 -> 0; matrix products, arithmetic and copies ran while one was open for 2% -> 0% of each run, Pallas kernels for 0% -> 0%
where the time goes in v1:
time: 104 us; the launch traced here: 102 us
  Pallas kernels  97.5 us (94%)
  local copies, waits for them, and re-layouts  4.21 us (4%)
    pallas_call x1, Pallas kernels, body(): pl.pallas_call(kernel, out_shape=(jax.ShapeDtypeStruct((SNAPS, MODES), F3...  97.5 us
    unnamed x3, local copies, waits for them, and re-layouts  4.21 us

profile of v1, /device:TPU:6, one launch (start us, length us, event | category | flops | bytes accessed | tf_op | source)
XLA Modules:
  0.0 102.4 jit_solution(10171599663362179436)
XLA Ops:
  0.6 1.3 %copy.10.stoich = s32[8,4]{1,0:T(8,128)} copy(s32[8,4]{0,1:T(4,128)} %param.13) | data formatting | bytes 256 | tf_op args[5]
  2.0 97.5 %shard_map.95 = (f32[8,256]{1,0:T(8,128)}, f32[4,4,16,128]{3,2,1,0:T(8,128)}) custom-call(f32[4,4,16,128]{3,2,1,0:T(8,128)} %terminal.1, f32[4]{0:T(128)} %diffusion.1, f32[4,16,128]{2,1,0:T(8,128)} %velocity.1, s32[4,16,128]{2,1,0:T(8,128)} %material.1, f32[8,8]{1,0:T(8,128)} %rates.1, s32[8,4]{1,0:T(8,128)} %copy.10.stoich, s32[8]{0:T(128)} %plan.1, ...), custom_call_target="tpu_custom_call" | custom-call | tf_op jit(solution)/shard_map/pallas_call | solution.py:535
  99.5 1.3 %copy.13 = f32[8,256]{1,0:T(8,128)} copy(f32[8,256]{1,0:T(8,128)} %get-tuple-element.4) | data formatting | bytes 16384
  100.8 1.6 %copy.14 = f32[4,4,16,128]{3,2,1,0:T(8,128)} copy(f32[4,4,16,128]{3,2,1,0:T(8,128)} %get-tuple-element.5) | data formatting | bytes 262144

commit v2 on v1

--- a/solution.py
+++ b/solution.py
@@ -31,8 +31,8 @@
     terminal, diffusion, velocity, material, rates, stoich, plan, basis,
     coeff_out, adj_out,
     bv, st, fields, rx, ry, rz, pack, edge, cx, cy, cz, lam, mid,
-    kc, vm, dm, rc, gram, got, proj, suma, sumb,
-    basis_sem, hs, hr, cs, cr, as_, ar, ss, sr,
+    kc, vm, dm, rc, gram, got, proj, suma, sumb, gparts, gsums, gfull,
+    basis_sem, hs, hr, cs, cr, as_, ar, ss, sr, gs, gr,
 ):
     g = lax.axis_index("grp")
     x = lax.axis_index("gx")
@@ -113,7 +113,7 @@
             src = st.at[n, :, :, pl.ds(0 if i == 2 else 8, 8), :]
             dst = ry.at[par, i - 2]
         elif i < 6:
-            src = st.at[n]
+            src = pack.at[par, 5]
             dst = rz.at[par, i - 4]
         else:
             if i < 10:
@@ -156,6 +156,15 @@
                 hit = jnp.logical_or(lane == i, lane == (i - 1) % CZ)
                 acc = jnp.where(hit, pltpu.roll(v, i, 1) if i else v, acc)
         pack[par, 4] = acc
+        acc = jnp.zeros((8, CZ), F32)
+        for s in range(SPEC):
+            for p in range(CX):
+                for t in range(2):
+                    i = 4 * ((s * CX + p) * 2 + t)
+                    v = st[n, s, p, t * 8:(t + 1) * 8, :]
+                    place = lax.rem(lane + (CZ + 2 - i), CZ)
+                    acc = jnp.where(place < 4, pltpu.roll(v, i, 1) if i else v, acc)
+        pack[par, 5] = acc
 
     def start_halo(k, par):
         pack_edges(k, par)
@@ -190,14 +199,23 @@
 
     def unpack(par):
         zero8 = jnp.zeros((8, CZ), F32)
+        far = lax.rem(lane, 4) >= 2
+        comb = jnp.where(
+            jnp.logical_and(far, lane < low(zm, CZ)), rz[par, 1],
+            jnp.where(
+                jnp.logical_and(jnp.logical_not(far), lane < low(zp, CZ)), rz[par, 0], zero8))
+        for s in range(SPEC):
+            for p in range(CX):
+                for t in range(2):
+                    i = 4 * ((s * CX + p) * 2 + t)
+                    tile = pltpu.roll(comb, (CZ - i) % CZ, 1) if i else comb
+                    lam[s, 2 + p, t * 8:(t + 1) * 8, 128:256] = tile
         for s in range(SPEC):
             lam[s, 0:2, 0:16, 0:128] = jnp.where(xm, rx[par, 1, s], 0.0)
             lam[s, 6:8, 0:16, 0:128] = jnp.where(xp, rx[par, 0, s], 0.0)
             for p in range(CX):
                 lam[s, 2 + p, 16:24, 0:128] = jnp.where(
                     y_from_p, ry[par, 0, s, p], jnp.where(y_from_m, ry[par, 1, s, p], zero8))
-                lam[s, 2 + p, 0:16, 128:256] = jnp.where(
-                    z_from_p, rz[par, 0, s, p], jnp.where(z_from_m, rz[par, 1, s, p], 0.0))
 
         def flag(a, b):
             return jnp.logical_and(a, b)
@@ -320,8 +338,8 @@
                 for a in range(SPEC):
                     dm[a, p, r0:r1, l0:l1] = inside * diffusion[a]
                     for b in range(SPEC):
-                        v = (looked[a] * stoich[a, b].astype(F32)
-                             + looked[a + 4] * stoich[a + 4, b].astype(F32))
+                        v = (looked[a] * stoich[b, a].astype(F32)
+                             + looked[a + 4] * stoich[b, a + 4].astype(F32))
                         if a == b:
                             kc[a, p, r0:r1, l0:l1] = (
                                 inside * (1.0 - 6.0 * diffusion[a]) - vel + v)
@@ -378,13 +396,61 @@
         rows = 512
 
         def one(c, carry):
-            at = pl.multiple_of(k * PART + c * rows, rows)
+            at = pl.multiple_of(k * 2 * PART + c * rows, rows)
             block = bv[pl.ds(at, rows), :]
             gram[...] += lax.dot_general(
                 block, block, (((0,), (0,)), ((), ())), preferred_element_type=F32)
             return carry
 
-        lax.fori_loop(0, PART // rows, one, 0)
+        lax.fori_loop(0, 2 * PART // rows, one, 0)
+
+    slab = MODES // (n_g * n_y)
+
+    def slab_of(q):
+        return pl.ds(pl.multiple_of(q * slab, slab), slab)
+
+    def gram_a(o):
+        q, where = group_a(o)
+        return pltpu.make_async_remote_copy(
+            src_ref=gram.at[slab_of(q), :], dst_ref=gparts.at[ga],
+            send_sem=gs.at[0, o], recv_sem=gr.at[0, o], device_id=where, device_id_type=MESH)
+
+    def gram_b(o):
+        q, where = group_b(o)
+        return pltpu.make_async_remote_copy(
+            src_ref=gsums.at[x], dst_ref=gsums.at[x],
+            send_sem=gs.at[1, o], recv_sem=gr.at[1, o], device_id=where, device_id_type=MESH)
+
+    def gram_c(o):
+        q, where = group_a(o)
+        return pltpu.make_async_remote_copy(
+            src_ref=gfull.at[slab_of(ga), :], dst_ref=gfull.at[slab_of(ga), :],
+            send_sem=gs.at[2, o], recv_sem=gr.at[2, o], device_id=where, device_id_type=MESH)
+
+    def gram_start():
+        gparts[ga] = gram[slab_of(ga), :]
+        for o in range(1, n_g * n_y):
+            gram_a(o).start()
+
+    def gram_middle():
+        for o in range(1, n_g * n_y):
+            gram_a(o).wait_recv()
+        total = gparts[0]
+        for q in range(1, n_g * n_y):
+            total = total + gparts[q]
+        gsums[x] = total
+        for o in range(1, n_x):
+            gram_b(o).start()
+
+    def gram_last():
+        for o in range(1, n_x):
+            gram_b(o).wait_recv()
+        total = gsums[0]
+        for q in range(1, n_x):
+            total = total + gsums[q]
+        gfull[slab_of(ga), :] = total
+        for o in range(1, n_g * n_y):
+            gram_c(o).start()
 
     start_halo(0, 0)
     for i in range(6):
@@ -404,8 +470,24 @@
             for o in range(1, n_g):
                 snap_copy(k - 1, o).start()
 
-        basis_copy(k).wait()
-        gram_part(k)
+        @pl.when(k < ROUNDS // 2)
+        def _():
+            basis_copy(2 * k).wait()
+            basis_copy(2 * k + 1).wait()
+            gram_part(k)
+
+        @pl.when(k == ROUNDS // 2)
+        def _():
+            gram_start()
+
+        @pl.when(k == ROUNDS // 2 + 1)
+        def _():
+            gram_middle()
+
+        @pl.when(k == ROUNDS // 2 + 2)
+        def _():
+            gram_last()
+
         wait_halo(k, par)
         unpack(par)
         first_step()
@@ -424,76 +506,78 @@
         def _(i=i):
             coeff_copy(i).wait_send()
 
-    def snap_wait(k, carry):
-        for o in range(1, n_g):
-            snap_copy(k, o).wait_recv()
-        return carry
-
-    lax.fori_loop(0, ROUNDS, snap_wait, 0)
-
     flat = got.reshape(STEPS * 4 * ROWS, CZ)
     proj[...] = jnp.zeros_like(proj)
-
-    def project(c, carry):
-        total = jnp.zeros((2 * STEPS, MODES), F32)
-        for u in range(4):
-            at = c * 4 + u
-            vals = [flat[pl.ds(zq * ROWS + at, STEPS, stride=4 * ROWS), :] for zq in range(4)]
+    unroll = 8
+
+    def project(zq):
+        def one(c, carry):
+            vals, blocks = [], []
+            for u in range(unroll):
+                at = c * unroll + u
+                vals.append(flat[pl.ds(zq * ROWS + at, STEPS, stride=4 * ROWS), :])
+                blocks.append(
+                    bv[pl.ds(pl.multiple_of(at * 512 + zq * CZ, CZ), CZ), :])
             a = jnp.concatenate(vals, axis=1)
             hi = a.astype(BF16)
             lo = (a - hi.astype(F32)).astype(BF16)
             both = jnp.concatenate([hi, lo], axis=0)
-            rows = pl.ds(pl.multiple_of(at * 512, 512), 512)
-            total += jnp.dot(both, bv[rows, :], preferred_element_type=F32)
-        proj[...] += total
-        return carry
-
-    lax.fori_loop(0, ROWS // 4, project, 0)
+            proj[...] += jnp.dot(
+                both, jnp.concatenate(blocks, axis=0), preferred_element_type=F32)
+            return carry
+
+        lax.fori_loop(0, ROWS // unroll, one, 0)
+
+    project(g)
+    for o in (1, 3, 2):
+        def snap_wait(k, carry, o=o):
+            snap_copy(k, o).wait_recv()
+            return carry
+
+        lax.fori_loop(0, ROUNDS, snap_wait, 0)
+        project(lax.rem(g + n_g - o, n_g))
 
     slot = lax.broadcasted_iota(jnp.int32, (SNAPS, MODES), 0)
     step_of = jnp.zeros((SNAPS, MODES), jnp.int32)
     for j in range(SNAPS):
         step_of = jnp.where(slot == j, plan[j], step_of)
     first = jnp.zeros((SNAPS, MODES), F32)
-    rest = jnp.zeros((SNAPS, MODES), F32)
     for n in range(STEPS):
-        hit = step_of == n
-        first = jnp.where(hit, jnp.broadcast_to(proj[n:n + 1, :], first.shape), first)
-        rest = jnp.where(
-            hit, jnp.broadcast_to(proj[STEPS + n:STEPS + n + 1, :], first.shape), rest)
-
-    def all_sum(value, turn):
-        suma[turn, ga] = value
+        row = proj[n:n + 1, :] + proj[STEPS + n:STEPS + n + 1, :]
+        first = jnp.where(step_of == n, jnp.broadcast_to(row, first.shape), first)
+
+    def all_sum(value):
+        suma[ga] = value
 
         def a_copy(o):
             q, where = group_a(o)
             return pltpu.make_async_remote_copy(
-                src_ref=suma.at[turn, ga], dst_ref=suma.at[turn, ga],
-                send_sem=ss.at[turn, 0, o], recv_sem=sr.at[turn, 0, o],
+                src_ref=suma.at[ga], dst_ref=suma.at[ga],
+                send_sem=ss.at[0, o], recv_sem=sr.at[0, o],
                 device_id=where, device_id_type=MESH)
 
         def b_copy(o):
             q, where = group_b(o)
             return pltpu.make_async_remote_copy(
-                src_ref=sumb.at[turn, x], dst_ref=sumb.at[turn, x],
-                send_sem=ss.at[turn, 1, o], recv_sem=sr.at[turn, 1, o],
+                src_ref=sumb.at[x], dst_ref=sumb.at[x],
+                send_sem=ss.at[1, o], recv_sem=sr.at[1, o],
                 device_id=where, device_id_type=MESH)
 
         for o in range(1, n_g * n_y):
             a_copy(o).start()
         for o in range(1, n_g * n_y):
             a_copy(o).wait_recv()
-        total = suma[turn, 0]
+        total = suma[0]
         for q in range(1, n_g * n_y):
-            total = total + suma[turn, q]
-        sumb[turn, x] = total
+            total = total + suma[q]
+        sumb[x] = total
         for o in range(1, n_x):
             b_copy(o).start()
         for o in range(1, n_x):
             b_copy(o).wait_recv()
-        total = sumb[turn, 0]
+        total = sumb[0]
         for q in range(1, n_x):
-            total = total + sumb[turn, q]
+            total = total + sumb[q]
 
         def finish():
             for o in range(1, n_g * n_y):
@@ -503,9 +587,11 @@
 
         return total, finish
 
-    total, finish_0 = all_sum(first, 0)
+    total, finish = all_sum(first)
     low_first = total.astype(BF16)
-    gm = gram[...]
+    for o in range(1, n_g * n_y):
+        gram_c(o).wait_recv()
+    gm = gfull[...]
     g1 = gm.astype(BF16)
     left = gm - g1.astype(F32)
     g2 = left.astype(BF16)
@@ -513,11 +599,13 @@
     back = jnp.dot(low_first, g1, preferred_element_type=F32)
     back += jnp.dot(low_first, g2, preferred_element_type=F32)
     back += jnp.dot(low_first, g3, preferred_element_type=F32)
-    second = (first - back) + rest
-    more, finish_1 = all_sum(second, 1)
-    coeff_out[...] = total + more
-    finish_0()
-    finish_1()
+    coeff_out[...] = total + (total - back)
+    finish()
+    for o in range(1, n_g * n_y):
+        gram_a(o).wait_send()
+        gram_c(o).wait_send()
+    for o in range(1, n_x):
+        gram_b(o).wait_send()
 
     def snap_sent(k, carry):
         for o in range(1, n_g):
@@ -546,8 +634,8 @@
             v((2, CX, CY, CZ), F32),
             v((2, 2, SPEC, 2, CY, CZ), F32),
             v((2, 2, SPEC, CX, 8, CZ), F32),
-            v((2, 2, SPEC, CX, CY, CZ), F32),
-            v((2, 5, 8, CZ), F32),
+            v((2, 2, 8, CZ), F32),
+            v((2, 6, 8, CZ), F32),
             v((2, 12, 8, CZ), F32),
             v((2, 2, 1, CY, CZ), F32),
             v((2, 2, CX, 8, CZ), F32),
@@ -561,8 +649,11 @@
             v((MODES, MODES), F32),
             v((STEPS, 4, CX, CY, CZ), F32),
             v((2 * STEPS, MODES), F32),
-            v((2, 16, SNAPS, MODES), F32),
-            v((2, 8, SNAPS, MODES), F32),
+            v((16, SNAPS, MODES), F32),
+            v((8, SNAPS, MODES), F32),
+            v((16, 16, MODES), F32),
+            v((8, 16, MODES), F32),
+            v((MODES, MODES), F32),
             dma((ROUNDS,)),
             dma((2, 18)),
             dma((2, 18)),
@@ -570,14 +661,16 @@
             dma((6,)),
             dma((ROUNDS, 3)),
             dma((ROUNDS, 3)),
-            dma((2, 2, 16)),
-            dma((2, 2, 16)),
+            dma((2, 16)),
+            dma((2, 16)),
+            dma((3, 16)),
+            dma((3, 16)),
         ],
         compiler_params=pltpu.CompilerParams(
             collective_id=0, has_side_effects=True, vmem_limit_bytes=60 * 1024 * 1024
         ),
     )(
-        terminal, diffusion, velocity, material, rates, stoich, plan,
+        terminal, diffusion, velocity, material, rates, stoich.T, plan,
         basis.reshape(BASIS_ROWS, MODES),
     )
 

time: 104 us -> 92.6 us (0.89); the launches traced: 102 us -> 92.5 us
  Pallas kernels: 97.5 us -> 89 us
  local copies, waits for them, and re-layouts: 4.21 us -> 2.86 us
    pallas_call x1, Pallas kernels: 97.5 us -> 89 us  [body(): pl.pallas_call(kernel, out_shape=(jax.ShapeDtypeStruct((SNAPS, MODES), F3...]
    unnamed x3 -> x2, local copies, waits for them, and re-layouts: 4.21 us -> 2.86 us
where the time goes in v2:
time: 92.6 us; the launch traced here: 92.5 us
  Pallas kernels  89 us (96%)
  local copies, waits for them, and re-layouts  2.86 us (3%)
    pallas_call x1, Pallas kernels, body(): pl.pallas_call(kernel, out_shape=(jax.ShapeDtypeStruct((SNAPS, MODES), F3...  89 us
    unnamed x2, local copies, waits for them, and re-layouts  2.86 us

profile of v2, /device:TPU:6, one launch (start us, length us, event | category | flops | bytes accessed | tf_op | source)
XLA Modules:
  0.0 92.5 jit_solution(8176898870902858265)
XLA Ops:
  0.6 89.0 %shard_map.95 = (f32[8,256]{1,0:T(8,128)}, f32[4,4,16,128]{3,2,1,0:T(8,128)}) custom-call(f32[4,4,16,128]{3,2,1,0:T(8,128)} %terminal.1, f32[4]{0:T(128)} %diffusion.1, f32[4,16,128]{2,1,0:T(8,128)} %velocity.1, s32[4,16,128]{2,1,0:T(8,128)} %material.1, f32[8,8]{1,0:T(8,128)} %rates.1, s32[4,8]{1,0:T(4,128)} %bitcast.3, s32[8]{0:T(128)} %plan.1, ...), custom_call_target="tpu_custom_call" | custom-call | tf_op jit(solution)/shard_map/pallas_call | solution.py:623
  89.6 1.3 %copy.12 = f32[8,256]{1,0:T(8,128)} copy(f32[8,256]{1,0:T(8,128)} %get-tuple-element.4) | data formatting | bytes 16384
  90.9 1.6 %copy.13 = f32[4,4,16,128]{3,2,1,0:T(8,128)} copy(f32[4,4,16,128]{3,2,1,0:T(8,128)} %get-tuple-element.5) | data formatting | bytes 262144

commit v3 on v2

--- a/solution.py
+++ b/solution.py
@@ -24,13 +24,13 @@
 XY = [(a, b, 0) for a in (-1, 1) for b in (-1, 1)]
 YZ = [(0, a, b) for a in (-1, 1) for b in (-1, 1)]
 DIRS = FACES + XZ + XY + YZ
-ORDER = [0, 1, 6, 7, 8, 9, 10, 11, 12, 13, 4, 5, 14, 15, 16, 17, 2, 3]
+ORDER = [6, 7, 8, 9, 10, 11, 12, 13, 0, 1, 14, 15, 16, 17, 4, 5, 2, 3]
 
 
 def kernel(
-    terminal, diffusion, velocity, material, rates, stoich, plan, basis,
-    coeff_out, adj_out,
-    bv, st, fields, rx, ry, rz, pack, edge, cx, cy, cz, lam, mid,
+    terminal_in, diffusion_in, velocity_in, material_in, rates_in, stoich_in, plan_in, basis,
+    coeff_to, adj_to,
+    diffusion, rates, stoich, plan, material, coeff_out, in_sem, out_sem, bv, st, fields, rx, ry, rz, pack, edge, cx, cy, cz, lam, mid,
     kc, vm, dm, rc, gram, got, proj, suma, sumb, gparts, gsums, gfull,
     basis_sem, hs, hr, cs, cr, as_, ar, ss, sr, gs, gr,
 ):
@@ -69,13 +69,17 @@
         rows = pl.ds(c * PART, PART)
         return pltpu.make_async_copy(basis.at[rows, :], bv.at[rows, :], basis_sem.at[c])
 
+    inputs = [
+        pltpu.make_async_copy(src, dst, in_sem.at[i]) for i, (src, dst) in enumerate((
+            (terminal_in, st.at[0]), (velocity_in, fields.at[0]), (material_in, material),
+            (diffusion_in, diffusion), (rates_in, rates), (stoich_in, stoich),
+            (plan_in, plan)))
+    ]
+    for copy in inputs:
+        copy.start()
     for c in range(ROUNDS):
         basis_copy(c).start()
 
-    st[0] = terminal[...]
-    fields[0] = velocity[...]
-    fields[1] = material[...].astype(F32)
-    lam[...] = jnp.zeros_like(lam)
 
     barrier = pltpu.get_barrier_semaphore()
     ga = g * n_y + y
@@ -101,6 +105,13 @@
         def _(d=d):
             pl.semaphore_signal(barrier, inc=1, device_id=dev(d), device_id_type=MESH)
 
+    lam[...] = jnp.zeros_like(lam)
+    mid[...] = jnp.zeros_like(mid)
+    gram[...] = jnp.zeros_like(gram)
+    for copy in inputs:
+        copy.wait()
+    fields[1] = material[...].astype(F32)
+    lam[:, 2:6, 0:16, 0:128] = st[0]
     pl.semaphore_wait(barrier, count)
 
     def halo_copy(i, k, par):
@@ -129,7 +140,7 @@
             device_id=dev(d), device_id_type=MESH,
         )
 
-    def pack_edges(k, par):
+    def pack_x_edges(k, par):
         n = 2 * k
         for side in (0, 1):
             plane = 0 if side == 0 else CX - 1
@@ -148,31 +159,38 @@
                 rows = jnp.where(hit, pltpu.roll(both, i, 0) if i else both, rows)
             pack[par, side] = acc
             pack[par, 2 + side] = rows
+
+    def pack_others(k, par):
+        n = 2 * k
         acc = jnp.zeros((8, CZ), F32)
+        face = jnp.zeros((8, CZ), F32)
         for s in range(SPEC):
             for p in range(CX):
+                t0 = st[n, s, p, 0:8, :]
+                t1 = st[n, s, p, 8:16, :]
                 i = 2 * (s * CX + p)
-                v = jnp.where(sub < 4, st[n, s, p, 0:8, :], st[n, s, p, 8:16, :])
+                v = jnp.where(sub < 4, t0, t1)
                 hit = jnp.logical_or(lane == i, lane == (i - 1) % CZ)
                 acc = jnp.where(hit, pltpu.roll(v, i, 1) if i else v, acc)
+                for t, v in ((0, t0), (1, t1)):
+                    i = 4 * ((s * CX + p) * 2 + t)
+                    place = lax.rem(lane + (CZ + 2 - i), CZ)
+                    face = jnp.where(place < 4, pltpu.roll(v, i, 1) if i else v, face)
         pack[par, 4] = acc
-        acc = jnp.zeros((8, CZ), F32)
-        for s in range(SPEC):
-            for p in range(CX):
-                for t in range(2):
-                    i = 4 * ((s * CX + p) * 2 + t)
-                    v = st[n, s, p, t * 8:(t + 1) * 8, :]
-                    place = lax.rem(lane + (CZ + 2 - i), CZ)
-                    acc = jnp.where(place < 4, pltpu.roll(v, i, 1) if i else v, acc)
-        pack[par, 5] = acc
+        pack[par, 5] = face
+
+    def send(i, k, par):
+        @pl.when(has(DIRS[i]))
+        def _():
+            halo_copy(i, k, par).start()
 
     def start_halo(k, par):
-        pack_edges(k, par)
-        for i in ORDER:
-
-            @pl.when(has(DIRS[i]))
-            def _(i=i):
-                halo_copy(i, k, par).start()
+        pack_x_edges(k, par)
+        for i in ORDER[:10]:
+            send(i, k, par)
+        pack_others(k, par)
+        for i in ORDER[10:]:
+            send(i, k, par)
 
     def wait_halo(k, par):
         for i in ORDER:
@@ -292,16 +310,14 @@
             device_id=(q, x, y), device_id_type=MESH,
         )
 
-    gram[...] = jnp.zeros_like(gram)
-    lam[:, 2:6, 0:16, 0:128] = terminal[...]
-
-    def coefficients():
-        sub24 = lax.broadcasted_iota(jnp.int32, (24, 256), 0)
-        lane24 = lax.broadcasted_iota(jnp.int32, (24, 256), 1)
+
+    def coefficients(outer):
         for p in range(6):
             own = 1 <= p <= CX
             for r0, r1, l0, l1 in ((0, 16, 0, 128), (16, 24, 0, 128), (0, 16, 128, 256)):
                 if not own and (r0, l0) != (0, 0):
+                    continue
+                if outer == (own and (r0, l0) == (0, 0)):
                     continue
                 vals = []
                 for f in range(2):
@@ -390,10 +406,10 @@
                 st[n + 2, s, p - 1] = new
                 lam[s, p + 1, 0:16, 0:128] = new
 
-    mid[...] = jnp.zeros_like(mid)
-
     def gram_part(k):
         rows = 512
+        basis_copy(2 * k).wait()
+        basis_copy(2 * k + 1).wait()
 
         def one(c, carry):
             at = pl.multiple_of(k * 2 * PART + c * rows, rows)
@@ -453,13 +469,15 @@
             gram_c(o).start()
 
     start_halo(0, 0)
+    coefficients(False)
+    gram_part(0)
     for i in range(6):
 
         @pl.when(has(minus(DIRS[i])))
         def _(i=i):
             coeff_copy(i).wait_recv()
 
-    coefficients()
+    coefficients(True)
 
     def round_(k, carry):
         par = lax.rem(k, 2)
@@ -470,10 +488,8 @@
             for o in range(1, n_g):
                 snap_copy(k - 1, o).start()
 
-        @pl.when(k < ROUNDS // 2)
+        @pl.when(jnp.logical_and(k > 0, k < ROUNDS // 2))
         def _():
-            basis_copy(2 * k).wait()
-            basis_copy(2 * k + 1).wait()
             gram_part(k)
 
         @pl.when(k == ROUNDS // 2)
@@ -499,7 +515,8 @@
     lax.fori_loop(0, ROUNDS, round_, 0)
     for o in range(1, n_g):
         snap_copy(ROUNDS - 1, o).start()
-    adj_out[...] = st[STEPS]
+    adj_copy = pltpu.make_async_copy(st.at[STEPS], adj_to, out_sem.at[0])
+    adj_copy.start()
     for i in range(6):
 
         @pl.when(has(DIRS[i]))
@@ -600,6 +617,8 @@
     back += jnp.dot(low_first, g2, preferred_element_type=F32)
     back += jnp.dot(low_first, g3, preferred_element_type=F32)
     coeff_out[...] = total + (total - back)
+    coeff_copy_out = pltpu.make_async_copy(coeff_out, coeff_to, out_sem.at[1])
+    coeff_copy_out.start()
     finish()
     for o in range(1, n_g * n_y):
         gram_a(o).wait_send()
@@ -613,11 +632,12 @@
         return carry
 
     lax.fori_loop(0, ROUNDS, snap_sent, 0)
+    adj_copy.wait()
+    coeff_copy_out.wait()
 
 
 def body(terminal, diffusion, velocity, material, rates, stoich, plan, basis):
-    vmem = pl.BlockSpec(memory_space=pltpu.VMEM)
-    smem = pl.BlockSpec(memory_space=pltpu.SMEM)
+    sm = pltpu.SMEM
     dma = pltpu.SemaphoreType.DMA
     v = pltpu.VMEM
     return pl.pallas_call(
@@ -626,9 +646,17 @@
             jax.ShapeDtypeStruct((SNAPS, MODES), F32),
             jax.ShapeDtypeStruct((SPEC, CX, CY, CZ), F32),
         ),
-        in_specs=[vmem, smem, vmem, vmem, smem, smem, smem, pl.BlockSpec(memory_space=pl.ANY)],
-        out_specs=(vmem, vmem),
+        in_specs=[pl.BlockSpec(memory_space=pl.ANY)] * 8,
+        out_specs=(pl.BlockSpec(memory_space=pl.ANY),) * 2,
         scratch_shapes=[
+            sm((SPEC,), F32),
+            sm((MATS, 8), F32),
+            sm((SPEC, 8), jnp.int32),
+            sm((SNAPS,), jnp.int32),
+            v((CX, CY, CZ), jnp.int32),
+            v((SNAPS, MODES), F32),
+            dma((7,)),
+            dma((2,)),
             v((BASIS_ROWS, MODES), BF16),
             v((STEPS + 1, SPEC, CX, CY, CZ), F32),
             v((2, CX, CY, CZ), F32),

time: 92.6 us -> 83.1 us (0.90)
  Pallas kernels: 89 us -> 79.4 us
    pallas_call x1, Pallas kernels: 89 us -> 79.4 us  [body(): pl.pallas_call(kernel, out_shape=(jax.ShapeDtypeStruct((SNAPS, MODES), F3...]
where the time goes in v3:
time: 83.1 us; the launch traced here: 82.9 us
  Pallas kernels  79.4 us (96%)
  local copies, waits for them, and re-layouts  2.86 us (3%)
    pallas_call x1, Pallas kernels, body(): pl.pallas_call(kernel, out_shape=(jax.ShapeDtypeStruct((SNAPS, MODES), F3...  79.4 us
    unnamed x2, local copies, waits for them, and re-layouts  2.86 us

profile of v3, /device:TPU:6, one launch (start us, length us, event | category | flops | bytes accessed | tf_op | source)
XLA Modules:
  0.0 82.9 jit_solution(4195552278746154526)
XLA Ops:
  0.6 79.4 %shard_map.95 = (f32[8,256]{1,0:T(8,128)}, f32[4,4,16,128]{3,2,1,0:T(8,128)}) custom-call(f32[4,4,16,128]{3,2,1,0:T(8,128)} %terminal_in.1, f32[4]{0:T(128)} %diffusion_in.1, f32[4,16,128]{2,1,0:T(8,128)} %velocity_in.1, s32[4,16,128]{2,1,0:T(8,128)} %material_in.1, f32[8,8]{1,0:T(8,128)} %rates_in.1, s32[4,8]{1,0:T(4,128)} %bitcast.3, s32[8]{0:T(128)} %plan_in.1, ...), custom_call_target="tpu_custom_call" | custom-call | tf_op jit(solution)/shard_map/pallas_call | solution.py:643
  80.0 1.3 %copy.12 = f32[8,256]{1,0:T(8,128)} copy(f32[8,256]{1,0:T(8,128)} %get-tuple-element.4) | data formatting | bytes 16384
  81.3 1.6 %copy.13 = f32[4,4,16,128]{3,2,1,0:T(8,128)} copy(f32[4,4,16,128]{3,2,1,0:T(8,128)} %get-tuple-element.5) | data formatting | bytes 262144

commit v4 on v3

--- a/solution.py
+++ b/solution.py
@@ -93,10 +93,6 @@
         return q, (g, q, y)
 
     count = jnp.int32(n_g * n_y - 1 + n_x - 1)
-    for o in range(1, n_g * n_y):
-        pl.semaphore_signal(barrier, inc=1, device_id=group_a(o)[1], device_id_type=MESH)
-    for o in range(1, n_x):
-        pl.semaphore_signal(barrier, inc=1, device_id=group_b(o)[1], device_id_type=MESH)
     for d in XZ + XY:
         cond = has(d)
         count = count + cond.astype(jnp.int32)
@@ -104,6 +100,11 @@
         @pl.when(cond)
         def _(d=d):
             pl.semaphore_signal(barrier, inc=1, device_id=dev(d), device_id_type=MESH)
+
+    for o in (4, 3, 5, 2, 6, 1, 7):
+        pl.semaphore_signal(barrier, inc=1, device_id=group_b(o)[1], device_id_type=MESH)
+    for o in range(1, n_g * n_y):
+        pl.semaphore_signal(barrier, inc=1, device_id=group_a(o)[1], device_id_type=MESH)
 
     lam[...] = jnp.zeros_like(lam)
     mid[...] = jnp.zeros_like(mid)
@@ -192,8 +193,8 @@
         for i in ORDER[10:]:
             send(i, k, par)
 
-    def wait_halo(k, par):
-        for i in ORDER:
+    def wait_halo(k, par, which):
+        for i in which:
 
             @pl.when(has(minus(DIRS[i])))
             def _(i=i):
@@ -215,70 +216,62 @@
     z_from_p = lane_full < low(zp, 64)
     z_from_m = lane_full >= high(zm, 64, CZ)
 
-    def unpack(par):
-        zero8 = jnp.zeros((8, CZ), F32)
+    def flag(a, b):
+        return jnp.logical_and(a, b)
+
+    even_lane = jnp.logical_not(odd_lane)
+    zero8 = jnp.zeros((8, CZ), F32)
+
+    def unpack_yz(par):
         far = lax.rem(lane, 4) >= 2
         comb = jnp.where(
-            jnp.logical_and(far, lane < low(zm, CZ)), rz[par, 1],
-            jnp.where(
-                jnp.logical_and(jnp.logical_not(far), lane < low(zp, CZ)), rz[par, 0], zero8))
+            flag(far, lane < low(zm, CZ)), rz[par, 1],
+            jnp.where(flag(jnp.logical_not(far), lane < low(zp, CZ)), rz[par, 0], zero8))
+        hi_m = flag(odd_lane, sub >= high(flag(ym, zm), 4, 8))
+        hi_p = flag(even_lane, sub >= high(flag(ym, zp), 4, 8))
+        lo_m = flag(odd_lane, sub < low(flag(yp, zm), 4))
+        lo_p = flag(even_lane, sub < low(flag(yp, zp), 4))
+        corner = jnp.where(hi_m, edge[par, 11], zero8)
+        corner = jnp.where(hi_p, edge[par, 10], corner)
+        corner = jnp.where(lo_m, edge[par, 9], corner)
+        corner = jnp.where(lo_p, edge[par, 8], corner)
         for s in range(SPEC):
             for p in range(CX):
+                lam[s, 2 + p, 16:24, 0:128] = jnp.where(
+                    y_from_p, ry[par, 0, s, p], jnp.where(y_from_m, ry[par, 1, s, p], zero8))
                 for t in range(2):
                     i = 4 * ((s * CX + p) * 2 + t)
                     tile = pltpu.roll(comb, (CZ - i) % CZ, 1) if i else comb
                     lam[s, 2 + p, t * 8:(t + 1) * 8, 128:256] = tile
+                i = 2 * (s * CX + p)
+                tile = pltpu.roll(corner, (CZ - i) % CZ, 1) if i else corner
+                lam[s, 2 + p, 16:24, 128:256] = tile
+
+    def unpack_x(par):
         for s in range(SPEC):
             lam[s, 0:2, 0:16, 0:128] = jnp.where(xm, rx[par, 1, s], 0.0)
             lam[s, 6:8, 0:16, 0:128] = jnp.where(xp, rx[par, 0, s], 0.0)
-            for p in range(CX):
-                lam[s, 2 + p, 16:24, 0:128] = jnp.where(
-                    y_from_p, ry[par, 0, s, p], jnp.where(y_from_m, ry[par, 1, s, p], zero8))
-
-        def flag(a, b):
-            return jnp.logical_and(a, b)
-
         for side, xh in ((1, xm), (0, xp)):
+            at = 1 if side == 1 else 6
             base = side * 2
-            m_m, m_p = edge[par, base + 1], edge[par, base]
             comb = jnp.where(
-                jnp.logical_and(odd_lane, lane < low(flag(xh, zm), CZ)), m_m,
+                flag(odd_lane, lane < low(flag(xh, zm), CZ)), edge[par, base + 1],
                 jnp.where(
-                    jnp.logical_and(jnp.logical_not(odd_lane), lane < low(flag(xh, zp), CZ)),
-                    m_p, zero8))
-            at = 1 if side == 1 else 6
+                    flag(even_lane, lane < low(flag(xh, zp), CZ)), edge[par, base], zero8))
+            base = 4 + side * 2
+            rows = jnp.where(
+                flag(odd_sub, sub < low(flag(xh, ym), 8)), edge[par, base + 1],
+                jnp.where(
+                    flag(jnp.logical_not(odd_sub), sub < low(flag(xh, yp), 8)),
+                    edge[par, base], zero8))
             for s in range(SPEC):
                 for t in range(2):
                     i = 2 * (s * 2 + t)
                     tile = pltpu.roll(comb, (CZ - i) % CZ, 1) if i else comb
                     lam[s, at, t * 8:(t + 1) * 8, 128:256] = tile
-        for side, xh in ((1, xm), (0, xp)):
-            base = 4 + side * 2
-            m_m, m_p = edge[par, base + 1], edge[par, base]
-            comb = jnp.where(
-                jnp.logical_and(odd_sub, sub < low(flag(xh, ym), 8)), m_m,
-                jnp.where(
-                    jnp.logical_and(jnp.logical_not(odd_sub), sub < low(flag(xh, yp), 8)),
-                    m_p, zero8))
-            at = 1 if side == 1 else 6
-            for s in range(SPEC):
                 i = 2 * s
-                tile = pltpu.roll(comb, (8 - i) % 8, 0) if i else comb
+                tile = pltpu.roll(rows, (8 - i) % 8, 0) if i else rows
                 lam[s, at, 16:24, 0:128] = tile
-        even_lane = jnp.logical_not(odd_lane)
-        hi_m = jnp.logical_and(odd_lane, sub >= high(flag(ym, zm), 4, 8))
-        hi_p = jnp.logical_and(even_lane, sub >= high(flag(ym, zp), 4, 8))
-        lo_m = jnp.logical_and(odd_lane, sub < low(flag(yp, zm), 4))
-        lo_p = jnp.logical_and(even_lane, sub < low(flag(yp, zp), 4))
-        comb = jnp.where(hi_m, edge[par, 11], zero8)
-        comb = jnp.where(hi_p, edge[par, 10], comb)
-        comb = jnp.where(lo_m, edge[par, 9], comb)
-        comb = jnp.where(lo_p, edge[par, 8], comb)
-        for s in range(SPEC):
-            for p in range(CX):
-                i = 2 * (s * CX + p)
-                tile = pltpu.roll(comb, (CZ - i) % CZ, 1) if i else comb
-                lam[s, 2 + p, 16:24, 128:256] = tile
 
     def coeff_copy(i):
         if i < 2:
@@ -294,12 +287,6 @@
             src_ref=src, dst_ref=dst, send_sem=cs.at[i], recv_sem=cr.at[i],
             device_id=dev(DIRS[i]), device_id_type=MESH,
         )
-
-    for i in range(6):
-
-        @pl.when(has(DIRS[i]))
-        def _(i=i):
-            coeff_copy(i).start()
 
     def snap_copy(k, o):
         q = lax.rem(g + o, n_g)
@@ -375,8 +362,8 @@
 
     own_tile = (0, 16, 0, 128)
 
-    def first_step():
-        for p in range(6):
+    def first_step(planes):
+        for p in planes:
             full = [lam[s, p + 1] for s in range(SPEC)]
             for s in range(SPEC):
                 c = full[s]
@@ -406,19 +393,17 @@
                 st[n + 2, s, p - 1] = new
                 lam[s, p + 1, 0:16, 0:128] = new
 
-    def gram_part(k):
-        rows = 512
-        basis_copy(2 * k).wait()
-        basis_copy(2 * k + 1).wait()
-
+    block_rows = 1024
+
+    def gram_blocks(start, count):
         def one(c, carry):
-            at = pl.multiple_of(k * 2 * PART + c * rows, rows)
-            block = bv[pl.ds(at, rows), :]
+            at = pl.multiple_of((start + c) * block_rows, block_rows)
+            block = bv[pl.ds(at, block_rows), :]
             gram[...] += lax.dot_general(
                 block, block, (((0,), (0,)), ((), ())), preferred_element_type=F32)
             return carry
 
-        lax.fori_loop(0, 2 * PART // rows, one, 0)
+        lax.fori_loop(0, count, one, 0)
 
     slab = MODES // (n_g * n_y)
 
@@ -469,8 +454,16 @@
             gram_c(o).start()
 
     start_halo(0, 0)
+    for i in range(6):
+
+        @pl.when(has(DIRS[i]))
+        def _(i=i):
+            coeff_copy(i).start()
+
     coefficients(False)
-    gram_part(0)
+    for c in range(2):
+        basis_copy(c).wait()
+    gram_blocks(0, 8)
     for i in range(6):
 
         @pl.when(has(minus(DIRS[i])))
@@ -488,32 +481,40 @@
             for o in range(1, n_g):
                 snap_copy(k - 1, o).start()
 
-        @pl.when(jnp.logical_and(k > 0, k < ROUNDS // 2))
+        @pl.when(k == 1)
         def _():
-            gram_part(k)
-
-        @pl.when(k == ROUNDS // 2)
+            for c in range(2, ROUNDS):
+                basis_copy(c).wait()
+
+        @pl.when(jnp.logical_and(k > 0, k < 5))
+        def _():
+            gram_blocks(2 + 6 * k, 6)
+
+        @pl.when(k == 5)
         def _():
             gram_start()
 
-        @pl.when(k == ROUNDS // 2 + 1)
+        @pl.when(k == 6)
         def _():
             gram_middle()
 
-        @pl.when(k == ROUNDS // 2 + 2)
+        @pl.when(k == 7)
         def _():
             gram_last()
 
-        wait_halo(k, par)
-        unpack(par)
-        first_step()
+        wait_halo(k, par, ORDER[10:])
+        unpack_yz(par)
+        first_step((2, 3))
+        wait_halo(k, par, ORDER[:10])
+        unpack_x(par)
+        first_step((0, 1, 4, 5))
         second_step(2 * k)
         wait_sent(k, par)
         got[pl.ds(2 * k, 2), g] = st[pl.ds(2 * k + 1, 2), g]
         return carry
 
     lax.fori_loop(0, ROUNDS, round_, 0)
-    for o in range(1, n_g):
+    for o in (2, 1, 3):
         snap_copy(ROUNDS - 1, o).start()
     adj_copy = pltpu.make_async_copy(st.at[STEPS], adj_to, out_sem.at[0])
     adj_copy.start()
@@ -525,10 +526,10 @@
 
     flat = got.reshape(STEPS * 4 * ROWS, CZ)
     proj[...] = jnp.zeros_like(proj)
-    unroll = 8
+    unroll = 16
 
     def project(zq):
-        def one(c, carry):
+        def one(c, total):
             vals, blocks = [], []
             for u in range(unroll):
                 at = c * unroll + u
@@ -539,11 +540,10 @@
             hi = a.astype(BF16)
             lo = (a - hi.astype(F32)).astype(BF16)
             both = jnp.concatenate([hi, lo], axis=0)
-            proj[...] += jnp.dot(
+            return total + jnp.dot(
                 both, jnp.concatenate(blocks, axis=0), preferred_element_type=F32)
-            return carry
-
-        lax.fori_loop(0, ROWS // unroll, one, 0)
+
+        proj[...] = lax.fori_loop(0, ROWS // unroll, one, proj[...])
 
     project(g)
     for o in (1, 3, 2):

time: 83.1 us -> 81.2 us (0.977)
  Pallas kernels: 79.4 us -> 77.6 us
    pallas_call x1, Pallas kernels: 79.4 us -> 77.6 us  [body(): pl.pallas_call(kernel, out_shape=(jax.ShapeDtypeStruct((SNAPS, MODES), F3...]
where the time goes in v4:
time: 81.2 us; the launch traced here: 81.1 us
  Pallas kernels  77.6 us (96%)
  local copies, waits for them, and re-layouts  2.86 us (4%)
    pallas_call x1, Pallas kernels, body(): pl.pallas_call(kernel, out_shape=(jax.ShapeDtypeStruct((SNAPS, MODES), F3...  77.6 us
    unnamed x2, local copies, waits for them, and re-layouts  2.86 us

profile of v4, /device:TPU:6, one launch (start us, length us, event | category | flops | bytes accessed | tf_op | source)
XLA Modules:
  0.0 81.1 jit_solution(3696830579312850207)
XLA Ops:
  0.6 77.6 %shard_map.95 = (f32[8,256]{1,0:T(8,128)}, f32[4,4,16,128]{3,2,1,0:T(8,128)}) custom-call(f32[4,4,16,128]{3,2,1,0:T(8,128)} %terminal_in.1, f32[4]{0:T(128)} %diffusion_in.1, f32[4,16,128]{2,1,0:T(8,128)} %velocity_in.1, s32[4,16,128]{2,1,0:T(8,128)} %material_in.1, f32[8,8]{1,0:T(8,128)} %rates_in.1, s32[4,8]{1,0:T(4,128)} %bitcast.3, s32[8]{0:T(128)} %plan_in.1, ...), custom_call_target="tpu_custom_call" | custom-call | tf_op jit(solution)/shard_map/pallas_call | solution.py:643
  78.2 1.3 %copy.12 = f32[8,256]{1,0:T(8,128)} copy(f32[8,256]{1,0:T(8,128)} %get-tuple-element.4) | data formatting | bytes 16384
  79.5 1.6 %copy.13 = f32[4,4,16,128]{3,2,1,0:T(8,128)} copy(f32[4,4,16,128]{3,2,1,0:T(8,128)} %get-tuple-element.5) | data formatting | bytes 262144

commit v5 on v4

--- a/solution.py
+++ b/solution.py
@@ -29,9 +29,9 @@
 
 def kernel(
     terminal_in, diffusion_in, velocity_in, material_in, rates_in, stoich_in, plan_in, basis,
-    coeff_to, adj_to,
+    joined,
     diffusion, rates, stoich, plan, material, coeff_out, in_sem, out_sem, bv, st, fields, rx, ry, rz, pack, edge, cx, cy, cz, lam, mid,
-    kc, vm, dm, rc, gram, got, proj, suma, sumb, gparts, gsums, gfull,
+    kc, vm, dm, rc, gram, got, proj, suma, sumb, gparts, gsums, gfull, gsplit,
     basis_sem, hs, hr, cs, cr, as_, ar, ss, sr, gs, gr,
 ):
     g = lax.axis_index("grp")
@@ -516,7 +516,8 @@
     lax.fori_loop(0, ROUNDS, round_, 0)
     for o in (2, 1, 3):
         snap_copy(ROUNDS - 1, o).start()
-    adj_copy = pltpu.make_async_copy(st.at[STEPS], adj_to, out_sem.at[0])
+    adj_copy = pltpu.make_async_copy(
+        st.at[STEPS], joined.at[pl.ds(0, SPEC)], out_sem.at[0])
     adj_copy.start()
     for i in range(6):
 
@@ -583,6 +584,15 @@
         for o in range(1, n_g * n_y):
             a_copy(o).start()
         for o in range(1, n_g * n_y):
+            gram_c(o).wait_recv()
+        gm = gfull[...]
+        g1 = gm.astype(BF16)
+        left = gm - g1.astype(F32)
+        g2 = left.astype(BF16)
+        gsplit[0] = g1
+        gsplit[1] = g2
+        gsplit[2] = (left - g2.astype(F32)).astype(BF16)
+        for o in range(1, n_g * n_y):
             a_copy(o).wait_recv()
         total = suma[0]
         for q in range(1, n_g * n_y):
@@ -606,18 +616,13 @@
 
     total, finish = all_sum(first)
     low_first = total.astype(BF16)
-    for o in range(1, n_g * n_y):
-        gram_c(o).wait_recv()
-    gm = gfull[...]
-    g1 = gm.astype(BF16)
-    left = gm - g1.astype(F32)
-    g2 = left.astype(BF16)
-    g3 = (left - g2.astype(F32)).astype(BF16)
-    back = jnp.dot(low_first, g1, preferred_element_type=F32)
-    back += jnp.dot(low_first, g2, preferred_element_type=F32)
-    back += jnp.dot(low_first, g3, preferred_element_type=F32)
-    coeff_out[...] = total + (total - back)
-    coeff_copy_out = pltpu.make_async_copy(coeff_out, coeff_to, out_sem.at[1])
+    back = jnp.dot(low_first, gsplit[0], preferred_element_type=F32)
+    back += jnp.dot(low_first, gsplit[1], preferred_element_type=F32)
+    back += jnp.dot(low_first, gsplit[2], preferred_element_type=F32)
+    result = total + (total - back)
+    coeff_out[0:SNAPS, :] = result[:, 0:CZ]
+    coeff_out[SNAPS:2 * SNAPS, :] = result[:, CZ:MODES]
+    coeff_copy_out = pltpu.make_async_copy(coeff_out, joined.at[SPEC, 0], out_sem.at[1])
     coeff_copy_out.start()
     finish()
     for o in range(1, n_g * n_y):
@@ -636,25 +641,44 @@
     coeff_copy_out.wait()
 
 
+def divide(joined, coeff_to, adj_to, field, coeff, sem):
+    lead = pltpu.make_async_copy(joined.at[pl.ds(0, SPEC)], field, sem.at[0])
+    tail = pltpu.make_async_copy(joined.at[SPEC, 0], coeff, sem.at[1])
+    lead.start()
+    tail.start()
+    tail.wait()
+    halves = [
+        pltpu.make_async_copy(
+            coeff.at[pl.ds(h * SNAPS, SNAPS), :], coeff_to.at[:, pl.ds(h * CZ, CZ)],
+            sem.at[2 + h])
+        for h in range(2)
+    ]
+    for half in halves:
+        half.start()
+    lead.wait()
+    last = pltpu.make_async_copy(field, adj_to, sem.at[4])
+    last.start()
+    for half in halves:
+        half.wait()
+    last.wait()
+
+
 def body(terminal, diffusion, velocity, material, rates, stoich, plan, basis):
     sm = pltpu.SMEM
     dma = pltpu.SemaphoreType.DMA
     v = pltpu.VMEM
-    return pl.pallas_call(
+    joined = pl.pallas_call(
         kernel,
-        out_shape=(
-            jax.ShapeDtypeStruct((SNAPS, MODES), F32),
-            jax.ShapeDtypeStruct((SPEC, CX, CY, CZ), F32),
-        ),
+        out_shape=jax.ShapeDtypeStruct((SPEC + 1, CX, CY, CZ), F32),
         in_specs=[pl.BlockSpec(memory_space=pl.ANY)] * 8,
-        out_specs=(pl.BlockSpec(memory_space=pl.ANY),) * 2,
+        out_specs=pl.BlockSpec(memory_space=pl.ANY),
         scratch_shapes=[
             sm((SPEC,), F32),
             sm((MATS, 8), F32),
             sm((SPEC, 8), jnp.int32),
             sm((SNAPS,), jnp.int32),
             v((CX, CY, CZ), jnp.int32),
-            v((SNAPS, MODES), F32),
+            v((CY, CZ), F32),
             dma((7,)),
             dma((2,)),
             v((BASIS_ROWS, MODES), BF16),
@@ -682,6 +706,7 @@
             v((16, 16, MODES), F32),
             v((8, 16, MODES), F32),
             v((MODES, MODES), F32),
+            v((3, MODES, MODES), BF16),
             dma((ROUNDS,)),
             dma((2, 18)),
             dma((2, 18)),
@@ -701,6 +726,17 @@
         terminal, diffusion, velocity, material, rates, stoich.T, plan,
         basis.reshape(BASIS_ROWS, MODES),
     )
+    return pl.pallas_call(
+        divide,
+        out_shape=(
+            jax.ShapeDtypeStruct((SNAPS, MODES), F32),
+            jax.ShapeDtypeStruct((SPEC, CX, CY, CZ), F32),
+        ),
+        in_specs=[pl.BlockSpec(memory_space=pl.ANY)],
+        out_specs=(pl.BlockSpec(memory_space=pl.ANY),) * 2,
+        scratch_shapes=[v((SPEC, CX, CY, CZ), F32), v((CY, CZ), F32), dma((5,))],
+        compiler_params=pltpu.CompilerParams(vmem_limit_bytes=60 * 1024 * 1024),
+    )(joined)
 
 
 def solution(mesh):

time: 81.2 us -> 79.9 us (0.984)
  local copies, waits for them, and re-layouts: 2.86 us -> 0 us
  Pallas kernels: 77.6 us -> 79.2 us
    unnamed x2 -> x0, local copies, waits for them, and re-layouts: 2.86 us -> none
    pallas_call x1 -> x2, Pallas kernels: 77.6 us -> 79.2 us  [the longest x1 77.5 us: body(): pl.pallas_call(kernel, out_shape=jax.ShapeDtypeStruct((SPEC + 1, CX, CY,...]
where the time goes in v5:
time: 79.9 us; the launch traced here: 79.8 us
  Pallas kernels  79.2 us (99%)
    pallas_call x1, Pallas kernels, body(): pl.pallas_call(kernel, out_shape=jax.ShapeDtypeStruct((SPEC + 1, CX, CY,...  77.5 us
    pallas_call x1, Pallas kernels, body(): pl.pallas_call(divide, out_shape=(jax.ShapeDtypeStruct((SNAPS, MODES), F3...  1.6 us

profile of v5, /device:TPU:6, one launch (start us, length us, event | category | flops | bytes accessed | tf_op | source)
XLA Modules:
  0.0 79.8 jit_solution(6849011376079097538)
XLA Ops:
  0.6 77.5 %shard_map.95.joined = f32[5,4,16,128]{3,2,1,0:T(8,128)} custom-call(f32[4,4,16,128]{3,2,1,0:T(8,128)} %terminal_in.1, f32[4]{0:T(128)} %diffusion_in.1, f32[4,16,128]{2,1,0:T(8,128)} %velocity_in.1, s32[4,16,128]{2,1,0:T(8,128)} %material_in.1, f32[8,8]{1,0:T(8,128)} %rates_in.1, s32[4,8]{1,0:T(4,128)} %bitcast.3, s32[8]{0:T(128)} %plan_in.1, ...), custom_call_target="tpu_custom_call" | custom-call | tf_op jit(solution)/shard_map/pallas_call | solution.py:670
  78.2 1.6 %shard_map.96 = (f32[8,256]{1,0:T(8,128)}, f32[4,4,16,128]{3,2,1,0:T(8,128)}) custom-call(f32[5,4,16,128]{3,2,1,0:T(8,128)} %shard_map.95.joined), custom_call_target="tpu_custom_call" | custom-call | tf_op jit(solution)/shard_map/pallas_call | solution.py:729

commit v6 on v5

--- a/solution.py
+++ b/solution.py
@@ -30,7 +30,7 @@
 def kernel(
     terminal_in, diffusion_in, velocity_in, material_in, rates_in, stoich_in, plan_in, basis,
     joined,
-    diffusion, rates, stoich, plan, material, coeff_out, in_sem, out_sem, bv, st, fields, rx, ry, rz, pack, edge, cx, cy, cz, lam, mid,
+    diffusion, rates, stoich, plan, material, coeff_out, in_sem, out_sem, bv, st, fields, rx, ry, rz, ypack, pack, edge, cx, cy, cz, lam, mid,
     kc, vm, dm, rc, gram, got, proj, suma, sumb, gparts, gsums, gfull, gsplit,
     basis_sem, hs, hr, cs, cr, as_, ar, ss, sr, gs, gr,
 ):
@@ -122,7 +122,7 @@
             src = st.at[n, :, pl.ds(0 if i == 0 else 2, 2)]
             dst = rx.at[par, i]
         elif i < 4:
-            src = st.at[n, :, :, pl.ds(0 if i == 2 else 8, 8), :]
+            src = ypack.at[par, i - 2]
             dst = ry.at[par, i - 2]
         elif i < 6:
             src = pack.at[par, 5]
@@ -179,6 +179,13 @@
                     face = jnp.where(place < 4, pltpu.roll(v, i, 1) if i else v, face)
         pack[par, 4] = acc
         pack[par, 5] = face
+        for s in range(SPEC):
+            for h in range(2):
+                a, b = 2 * h, 2 * h + 1
+                ypack[par, 0, s, h] = jnp.where(
+                    sub < 4, st[n, s, a, 0:8, :], pltpu.roll(st[n, s, b, 0:8, :], 4, 0))
+                ypack[par, 1, s, h] = jnp.where(
+                    sub >= 4, st[n, s, a, 8:16, :], pltpu.roll(st[n, s, b, 8:16, :], 4, 0))
 
     def send(i, k, par):
         @pl.when(has(DIRS[i]))
@@ -237,8 +244,11 @@
         corner = jnp.where(lo_p, edge[par, 8], corner)
         for s in range(SPEC):
             for p in range(CX):
+                t0, t1 = ry[par, 0, s, p // 2], ry[par, 1, s, p // 2]
+                if p % 2:
+                    t0, t1 = pltpu.roll(t0, 4, 0), pltpu.roll(t1, 4, 0)
                 lam[s, 2 + p, 16:24, 0:128] = jnp.where(
-                    y_from_p, ry[par, 0, s, p], jnp.where(y_from_m, ry[par, 1, s, p], zero8))
+                    y_from_p, t0, jnp.where(y_from_m, t1, zero8))
                 for t in range(2):
                     i = 4 * ((s * CX + p) * 2 + t)
                     tile = pltpu.roll(comb, (CZ - i) % CZ, 1) if i else comb
@@ -685,8 +695,9 @@
             v((STEPS + 1, SPEC, CX, CY, CZ), F32),
             v((2, CX, CY, CZ), F32),
             v((2, 2, SPEC, 2, CY, CZ), F32),
-            v((2, 2, SPEC, CX, 8, CZ), F32),
+            v((2, 2, SPEC, CX // 2, 8, CZ), F32),
             v((2, 2, 8, CZ), F32),
+            v((2, 2, SPEC, CX // 2, 8, CZ), F32),
             v((2, 6, 8, CZ), F32),
             v((2, 12, 8, CZ), F32),
             v((2, 2, 1, CY, CZ), F32),

time: 79.9 us -> 79.4 us (level)
  no operation moved by 1% of the time
where the time goes in v6:
time: 79.4 us; the launch traced here: 79.1 us
  Pallas kernels  78.5 us (99%)
    pallas_call x1, Pallas kernels, body(): pl.pallas_call(kernel, out_shape=jax.ShapeDtypeStruct((SPEC + 1, CX, CY,...  76.9 us
    pallas_call x1, Pallas kernels, body(): pl.pallas_call(divide, out_shape=(jax.ShapeDtypeStruct((SNAPS, MODES), F3...  1.6 us

profile of v6, /device:TPU:6, one launch (start us, length us, event | category | flops | bytes accessed | tf_op | source)
XLA Modules:
  0.0 79.1 jit_solution(8286749982454876633)
XLA Ops:
  0.6 76.9 %shard_map.95.joined = f32[5,4,16,128]{3,2,1,0:T(8,128)} custom-call(f32[4,4,16,128]{3,2,1,0:T(8,128)} %terminal_in.1, f32[4]{0:T(128)} %diffusion_in.1, f32[4,16,128]{2,1,0:T(8,128)} %velocity_in.1, s32[4,16,128]{2,1,0:T(8,128)} %material_in.1, f32[8,8]{1,0:T(8,128)} %rates_in.1, s32[4,8]{1,0:T(4,128)} %bitcast.3, s32[8]{0:T(128)} %plan_in.1, ...), custom_call_target="tpu_custom_call" | custom-call | tf_op jit(solution)/shard_map/pallas_call | solution.py:680
  77.5 1.6 %shard_map.96 = (f32[8,256]{1,0:T(8,128)}, f32[4,4,16,128]{3,2,1,0:T(8,128)}) custom-call(f32[5,4,16,128]{3,2,1,0:T(8,128)} %shard_map.95.joined), custom_call_target="tpu_custom_call" | custom-call | tf_op jit(solution)/shard_map/pallas_call | solution.py:740
